TPU v7x, 256 devices: a whole 4x4x8 slice. The times are simulated.
256 devices in a mesh: ctg: 32 (over x, y, core), br: 8 (over z).
Axes of the slice: x: 4, y: 4, z: 8, core: 2. Of those that a mesh axis runs over, the one named last changes fastest.
Arguments:
- base_vm: float32 [10240], P(('ctg', 'br')), may hold values from 0.95 to 1.05
- base_va: float32 [10240], P(('ctg', 'br')), may hold values from -0.6 to 0.6
- delta_state: float32 [256, 2, 10240], P('ctg', None, 'br'), may hold values from -0.18 to 0.18
- multipliers: float32 [256, 2, 10240], P('ctg', None, 'br'), may hold values from -6 to 6
- net_inj: float32 [256, 2, 10240], P('ctg', None, 'br'), may hold values from -6 to 6
- ang_grad: float32 [256, 10240], P('ctg', 'br'), may hold values from -6 to 6
- from_bus: int32 [13312], P('br'), may hold values from 0 to 10239
- to_bus: int32 [13312], P('br'), may hold values from 0 to 10239
- status: int32 [256, 13312], P('ctg', 'br'), may hold values 0 or 1
- conduct: float32 [13312], P('br'), may hold values from 1 to 5
- suscept: float32 [13312], P('br'), may hold values from -15 to -5
- charging: float32 [13312], P('br'), may hold values from 0.1 to 0.6
- rating: float32 [13312], P('br'), may hold values from 1 to 3
- slack: float32 [256, 13312], P('ctg', 'br'), may hold values from 0.05 to 2
- zdual: float32 [256, 13312], P('ctg', 'br'), may hold values from 0.05 to 2
Outputs:
- mismatch: float32 [256, 2, 10240], P('ctg', None, 'br')
- dual_res: float32 [256, 10240], P('ctg', 'br')
- limit_res: float32 [256, 13312], P('ctg', 'br')
- ctg_norms: float32 [256, 4], P('ctg')
- total_norms: float32 [4], replicated
All inputs are finite; a program needn't handle non-finite values. No bound on the sum of `status` on one device may be relied on, other than what follows from the above.
Results may differ from a plain program's by a relative error of at most 0.0003.
Values sent between devices are 32-bit elements; how exact they have to be, the bound alone decides.
A program may use at most 64 MiB of HBM per device.

v0:
```python
import functools

import jax
import jax.numpy as jnp
from jax import lax
from jax.experimental import pallas as pl
from jax.experimental.pallas import tpu as pltpu
from jax.sharding import PartitionSpec as P

LANES = 128
SPAN = 256
ROWS = 8
MESH = pl.DeviceIdType.MESH


def sin_cos(x):
    y = x * x
    sin_c = (1 / 6227020800, -1 / 39916800, 1 / 362880, -1 / 5040, 1 / 120, -1 / 6)
    cos_c = (-1 / 87178291200, 1 / 479001600, -1 / 3628800, 1 / 40320, -1 / 720, 1 / 24, -0.5)
    s = jnp.full_like(y, sin_c[0])
    for c in sin_c[1:]:
        s = s * y + c
    k = jnp.full_like(y, cos_c[0])
    for c in cos_c[1:]:
        k = k * y + c
    return x + x * y * s, 1.0 + y * k


def body(
    groups, ranks,
    base, delta, mult, net_any, ang_any, ends, params, rating, status3, status_any, slack_any, zdual_any,
    mis_out, dual_out, lim_out, norm_out, tot_out,
    bbuf, dbuf, mbuf, ebuf, pbuf, stbuf, table, acc,
    res, rbuf, flow, rflow, sqs, sqbuf, rowbuf,
    net, ang, status, slack, zdual, local,
    send, recv, base_send, base_recv, sq_send, sq_recv,
):
    grp, me = lax.axis_index("ctg"), lax.axis_index("br")
    count = groups * ranks
    mine = grp * ranks + me
    per = dbuf.shape[1]
    nb, nl = delta.shape[2], ends.shape[1]
    scen = delta.shape[0]

    own = pl.ds(me * per, per)
    local_copies = [
        pltpu.make_async_copy(a, b, local.at[i])
        for i, (a, b) in enumerate((
            (delta.at[own], dbuf.at[me]), (mult.at[own], mbuf.at[me]),
            (status_any, status), (slack_any, slack), (zdual_any, zdual),
            (net_any, net), (ang_any, ang),
        ))
    ]
    for copy in local_copies:
        copy.start()

    barrier = pltpu.get_barrier_semaphore()

    def greet(i, carry):
        peer = lax.rem(mine + i, count)
        pl.semaphore_signal(
            barrier, inc=1, device_id=(peer // ranks, lax.rem(peer, ranks)), device_id_type=MESH
        )
        return carry

    lax.fori_loop(1, count, greet, 0)
    pl.semaphore_wait(barrier, count - 1)

    def remote(src, dst, kind, step):
        return pltpu.make_async_remote_copy(
            src_ref=src, dst_ref=dst, send_sem=send.at[kind, step], recv_sem=recv.at[kind, step],
            device_id=(grp, lax.rem(me + step, ranks)), device_id_type=MESH,
        )

    def all_peers(slots, block, sends, recvs, i):
        peer = lax.rem(mine + i, count)
        return pltpu.make_async_remote_copy(
            src_ref=block, dst_ref=slots.at[mine], send_sem=sends.at[i], recv_sem=recvs.at[i],
            device_id=(peer // ranks, lax.rem(peer, ranks)), device_id_type=MESH,
        )

    def begin_base(i, c):
        all_peers(bbuf, base, base_send, base_recv, i).start()
        return c

    def finish_base(i, c):
        all_peers(bbuf, base, base_send, base_recv, i).wait()
        return c

    lax.fori_loop(1, count, begin_base, 0)
    first = []
    for step in range(1, ranks):
        peer = lax.rem(me + step, ranks)
        part = pl.ds(peer * per, per)
        first.append((
            remote(delta.at[part], dbuf.at[me], 0, step),
            remote(mult.at[part], mbuf.at[me], 1, step),
            remote(ends, ebuf.at[me], 2, step),
            remote(params, pbuf.at[me], 3, step),
            remote(status3.at[peer], stbuf.at[me], 4, step),
        ))
    for kind in range(5):
        for group in first:
            group[kind].start()

    bbuf[mine] = base[...]
    ebuf[me] = ends[...]
    pbuf[me] = params[...]
    stbuf[me] = status3[me]
    table[...] = jnp.zeros_like(table)
    acc[...] = jnp.zeros_like(acc)
    sqs[...] = jnp.zeros_like(sqs)
    for copy in local_copies:
        copy.wait()
    live_own = status[...].astype(jnp.float32)
    comp = live_own * (zdual[...] * slack[...] - 0.01)
    sqs[:, 3:4] = jnp.sum(comp * comp, axis=1, keepdims=True)

    lax.fori_loop(1, count, finish_base, 0)
    for group in first:
        for copy in group[:3]:
            copy.wait()

    for src in range(ranks):
        cols = slice(src * nb, (src + 1) * nb)
        volts = jnp.concatenate([bbuf[src * groups + i] for i in range(groups)], axis=1)
        for s in range(per):
            table[s : s + 1, cols] = volts[0:1] + dbuf[src, s, 0:1, :]
            table[per + s : per + s + 1, cols] = volts[1:2] + dbuf[src, s, 1:2, :]
            table[2 * per + s : 2 * per + s + 1, cols] = mbuf[src, s, 0:1, :]
            table[3 * per + s : 3 * per + s + 1, cols] = mbuf[src, s, 1:2, :]

    tiles = table.shape[1] // LANES
    high = table.shape[1] // SPAN

    chunk = SPAN if nl % SPAN == 0 else LANES
    pieces = nl // chunk
    bf16 = jnp.bfloat16

    def place(i):
        return lax.rem(me - i // pieces + ranks, ranks), pl.ds(pl.multiple_of(lax.rem(i, pieces) * chunk, chunk), chunk)

    def pick(i):
        src, cols = place(i)
        picked = []
        for end in range(2):
            spots = jnp.broadcast_to(ebuf[src, end : end + 1, cols], (ROWS, chunk))
            tiles_found = []
            for at in range(0, chunk, LANES):
                spot = spots[:, at : at + LANES]
                low, tile = spot & (LANES - 1), spot >> 7
                found = jnp.zeros((ROWS, LANES), jnp.float32)
                for k in range(tiles):
                    piece = jnp.take_along_axis(
                        table[:, k * LANES : (k + 1) * LANES], low, axis=1, mode="promise_in_bounds"
                    )
                    found = jnp.where(tile == k, piece, found)
                tiles_found.append(found)
            picked.append(jnp.concatenate(tiles_found, axis=1))
        return tuple(picked)

    def process(i, picked):
        src, cols = place(i)

        def quantity(end, q):
            return picked[end][q * per : (q + 1) * per, :]

        vf, vt = quantity(0, 0), quantity(1, 0)
        sn, cs = sin_cos(quantity(0, 1) - quantity(1, 1))
        par = pbuf[src, :, cols]
        g, b, h = par[0:1], par[1:2], par[2:3]
        live = stbuf[src, :, cols].astype(jnp.float32)
        u = vf * vt
        gc_bs, gc_mbs = g * cs + b * sn, g * cs - b * sn
        gs_bc, gs_mbc = g * sn + b * cs, g * sn - b * cs
        bh = -(b + h)
        pf = live * (g * vf * vf - u * gc_bs)
        qf = live * (bh * vf * vf - u * gs_mbc)
        pt = live * (g * vt * vt - u * gc_mbs)
        qt = live * (bh * vt * vt + u * gs_bc)
        fd = live * u * (
            quantity(0, 2) * gs_mbc - quantity(0, 3) * gc_bs
            + quantity(1, 2) * gs_bc + quantity(1, 3) * gc_mbs
        )
        flow[src, :, cols] = pf * pf + qf * qf
        blank = [jnp.zeros((ROWS - 3 * per, chunk), jnp.float32)]
        lefts, hots = [], []
        label = lax.broadcasted_iota(jnp.int32, (SPAN, chunk), 0).astype(bf16)
        for end, terms in ((0, [pf, qf, fd]), (1, [pt, qt, -fd])):
            value = jnp.concatenate(terms + blank, axis=0)
            head = value.astype(bf16).astype(jnp.float32)
            both = jnp.concatenate([head, value - head], axis=0).astype(bf16)
            spot = ebuf[src, end : end + 1, cols]
            row = jnp.broadcast_to(spot >> 8, (2 * ROWS, chunk)).astype(bf16)
            low = jnp.broadcast_to((spot & (SPAN - 1)), (2 * ROWS, chunk)).astype(bf16)
            low = jnp.concatenate([low] * (SPAN // (2 * ROWS)), axis=0)
            hots.append(jnp.where(low == label, bf16(1), bf16(0)))
            lefts.append(jnp.concatenate(
                [jnp.where(row == bf16(k), both, bf16(0)) for k in range(high)], axis=0
            ))
        acc[...] += lax.dot_general(
            jnp.concatenate(lefts, axis=1), jnp.concatenate(hots, axis=1),
            (((1,), (1,)), ((), ())), preferred_element_type=jnp.float32,
        )

    final = ranks * pieces - 1

    def one_step(step, picked):
        src = lax.rem(me - step + ranks, ranks)

        @pl.when(step > 0)
        def _():
            remote(params, pbuf.at[me], 3, step).wait()
            remote(status3.at[0], stbuf.at[me], 4, step).wait()

        def advance(t, picked):
            i = step * pieces + t
            following = pick(jnp.minimum(i + 1, final))
            process(i, picked)
            return following

        picked = lax.fori_loop(0, pieces, advance, picked)

        @pl.when(step > 0)
        def _():
            remote(flow.at[src], rflow.at[me], 6, ranks - step).start()

        return picked

    lax.fori_loop(0, ranks, one_step, pick(0))

    for k in range(high):
        at = k * SPAN
        row = k * 2 * ROWS
        sums = acc[row : row + ROWS, :] + acc[row + ROWS : row + 2 * ROWS, :]
        for q in range(3):
            res[at // nb, q, :, at % nb : at % nb + SPAN] = sums[q * per : (q + 1) * per, :]

    back = []
    for step in range(1, ranks):
        peer = lax.rem(me + step, ranks)
        back.append((
            remote(res.at[peer], rbuf.at[me], 5, step),
        ))
    for group in back:
        group[0].start()
    rbuf[me] = res[me]
    rflow[me] = flow[me]
    for step in range(1, ranks):
        remote(flow.at[me], rflow.at[me], 6, step).wait()
    for group in back:
        group[0].wait()

    rate = rating[...] * rating[...]
    for src in range(ranks):
        for s in range(per):
            c = src * per + s
            total = jnp.zeros((1, 1), jnp.float32)
            for k in range(2):
                row = rbuf[src, k, s : s + 1, :] - net[c, k : k + 1, :]
                mis_out[c, k : k + 1, :] = row
                total = total + jnp.sum(row * row, axis=1, keepdims=True)
            sqs[c : c + 1, 0:1] = total
        rows = slice(src * per, (src + 1) * per)
        dual = rbuf[src, 2] + ang[rows, :]
        dual_out[rows, :] = dual
        sqs[rows, 1:2] = jnp.sum(dual * dual, axis=1, keepdims=True)
        lim = status[rows, :].astype(jnp.float32) * (rflow[src] + slack[rows, :] - rate)
        lim_out[rows, :] = lim
        sqs[rows, 2:3] = jnp.sum(lim * lim, axis=1, keepdims=True)

    sqbuf[me] = sqs[...]
    near = [remote(sqbuf.at[me], sqbuf.at[me], 7, step) for step in range(1, ranks)]
    for copy in near:
        copy.start()
    for copy in near:
        copy.wait()
    group_sum = jnp.zeros((scen, LANES), jnp.float32)
    for z in range(ranks):
        group_sum = group_sum + sqbuf[z]
    norm_out[...] = jnp.sqrt(group_sum[:, 0:4])

    rowbuf[grp] = jnp.sum(group_sum, axis=0, keepdims=True)

    def across(i):
        return pltpu.make_async_remote_copy(
            src_ref=rowbuf.at[grp], dst_ref=rowbuf.at[grp],
            send_sem=sq_send.at[i], recv_sem=sq_recv.at[i],
            device_id=(lax.rem(grp + i, groups), me), device_id_type=MESH,
        )

    def begin(i, c):
        across(i).start()
        return c

    def finish(i, c):
        across(i).wait()
        return c

    lax.fori_loop(1, groups, begin, 0)
    lax.fori_loop(1, groups, finish, 0)

    def add(i, c):
        return c + rowbuf[i]

    everything = lax.fori_loop(0, groups, add, jnp.zeros((1, LANES), jnp.float32))
    tot_out[...] = jnp.sqrt(everything[:, 0:4] / (scen * groups))


def per_device(
    base_vm, base_va, delta_state, multipliers, net_inj, ang_grad, from_bus, to_bus,
    status, conduct, suscept, charging, rating, slack, zdual,
):
    groups, ranks = lax.axis_size("ctg"), lax.axis_size("br")
    count = groups * ranks
    scen, _, nb = delta_state.shape
    nl = from_bus.shape[0]
    per = scen // ranks
    buses = nb * ranks
    high = buses // SPAN
    base = jnp.stack([base_vm, base_va])
    ends = jnp.stack([from_bus, to_bus])
    params = jnp.stack([conduct, suscept, charging])
    f32 = jnp.float32
    vmem = pl.BlockSpec(memory_space=pltpu.VMEM)
    hbm = pl.BlockSpec(memory_space=pl.ANY)
    mis, dual, lim, norms, tot = pl.pallas_call(
        functools.partial(body, groups, ranks),
        out_shape=(
            jax.ShapeDtypeStruct((scen, 2, nb), f32),
            jax.ShapeDtypeStruct((scen, nb), f32),
            jax.ShapeDtypeStruct((scen, nl), f32),
            jax.ShapeDtypeStruct((scen, 4), f32),
            jax.ShapeDtypeStruct((1, 4), f32),
        ),
        in_specs=[vmem, hbm, hbm, hbm, hbm, vmem, vmem, vmem, vmem, hbm, hbm, hbm],
        out_specs=(vmem,) * 5,
        scratch_shapes=[
            pltpu.VMEM((count, 2, base_vm.shape[0]), f32),
            pltpu.VMEM((ranks, per, 2, nb), f32),
            pltpu.VMEM((ranks, per, 2, nb), f32),
            pltpu.VMEM((ranks, 2, nl), jnp.int32),
            pltpu.VMEM((ranks, 3, nl), f32),
            pltpu.VMEM((ranks, per, nl), jnp.int32),
            pltpu.VMEM((ROWS, buses), f32),
            pltpu.VMEM((high * 2 * ROWS, SPAN), f32),
            pltpu.VMEM((ranks, 3, per, nb), f32),
            pltpu.VMEM((ranks, 3, per, nb), f32),
            pltpu.VMEM((ranks, per, nl), f32),
            pltpu.VMEM((ranks, per, nl), f32),
            pltpu.VMEM((scen, LANES), f32),
            pltpu.VMEM((ranks, scen, LANES), f32),
            pltpu.VMEM((groups, 1, LANES), f32),
            pltpu.VMEM((scen, 2, nb), f32),
            pltpu.VMEM((scen, nb), f32),
            pltpu.VMEM((scen, nl), jnp.int32),
            pltpu.VMEM((scen, nl), f32),
            pltpu.VMEM((scen, nl), f32),
            pltpu.SemaphoreType.DMA((7,)),
            pltpu.SemaphoreType.DMA((8, ranks)),
            pltpu.SemaphoreType.DMA((8, ranks)),
            pltpu.SemaphoreType.DMA((count,)),
            pltpu.SemaphoreType.DMA((count,)),
            pltpu.SemaphoreType.DMA((count,)),
            pltpu.SemaphoreType.DMA((count,)),
        ],
        compiler_params=pltpu.CompilerParams(
            collective_id=0, has_side_effects=True, vmem_limit_bytes=48 << 20
        ),
    )(
        base, delta_state, multipliers, net_inj, ang_grad, ends, params, rating[None, :],
        status.reshape(ranks, per, nl), status, slack, zdual,
    )
    return (mis, dual, lim, norms, tot[0])


def solution(mesh):
    placed = (
        P(("ctg", "br")), P(("ctg", "br")),
        P("ctg", None, "br"), P("ctg", None, "br"), P("ctg", None, "br"), P("ctg", "br"),
        P("br"), P("br"), P("ctg", "br"), P("br"), P("br"), P("br"), P("br"),
        P("ctg", "br"), P("ctg", "br"),
    )
    return jax.shard_map(
        per_device,
        mesh=mesh,
        in_specs=placed,
        out_specs=(P("ctg", None, "br"), P("ctg", "br"), P("ctg", "br"), P("ctg", None), P()),
        check_vma=False,
    )
```

profile of v0, /device:TPU:1, one launch (start us, length us, event | category | flops | bytes accessed | tf_op | source)
XLA Modules:
  0.0 100.9 jit_solution(16842444387110879562)
XLA Ops:
  0.6 0.0 copy-start.10
  0.6 0.0 copy-start.7
  0.7 0.7 pad_maximum_fusion.1.base
  1.3 0.0 copy-start.8
  1.3 0.0 copy-start.9
  1.4 0.7 stack.33
  2.1 0.0 copy-done.7
  2.1 0.0 copy-start.2
  2.1 0.0 copy-done.8
  2.1 0.0 copy-start
  2.2 0.0 copy-done.9
  2.2 0.0 copy-done.10
  2.2 0.0 copy-start.1
  2.3 0.7 broadcast_in_dim.3.rating
  3.0 0.0 copy-done
  3.0 0.0 copy-done.2
  3.0 0.1 copy-done.1
  3.1 0.0 copy-start.3
  3.1 0.9 copy-done.3
  4.0 0.0 copy-start.4
  4.0 0.8 copy-done.4
  4.8 0.0 copy-start.5
  4.8 0.8 copy-done.5
  5.6 0.0 copy-start.6
  5.6 0.8 copy-done.6
  6.4 91.4 %shard_map.182 = (f32[8,2,1280]{2,1,0:T(2,128)S(1)}, f32[8,1280]{1,0:T(8,128)S(1)}, f32[8,1664]{1,0:T(8,128)S(1)}, f32[8,4]{1,0:T(8,128)S(1)}, f32[1,4]{1,0:T(1,128)S(1)}) custom-call(f32[2,40]{1,0:T(2,128)S(1)} %pad_maximum_fusion.1.base, f32[8,2,1280]{2,1,0:T(2,128)S(1)} %copy-done.1, f32[8,2,1280]{2,1,0:T(2,128)S(1)} %copy-done.2, ...), custom_call_target="tpu_custom_call" | custom-call | tf_op jit(solution)/shard_map/pallas_call | solution.py:327
  97.8 0.7 copy.20
  98.5 0.6 copy.25
  99.1 0.6 copy.26
  99.7 0.6 copy.27
  100.3 0.5 copy.28
  (7 shorter events, 0.1 us)
Async XLA Ops:
  0.6 1.6 %copy-start.10 = (f32[1664]{0:T(1024)S(1)}, f32[1664]{0:T(1024)}, u32[]{:S(2)}) copy-start(f32[1664]{0:T(1024)} %param.26) | copy-start | bytes 19972
  0.6 1.4 %copy-start.7 = (s32[1664]{0:T(1024)S(1)}, s32[1664]{0:T(1024)}, u32[]{:S(2)}) copy-start(s32[1664]{0:T(1024)} %param.22) | copy-start | bytes 19972
  1.3 0.8 copy-start.8
  1.3 0.8 copy-start.9
  2.1 0.9 copy-start.2
  2.1 0.8 copy-start
  2.2 0.9 copy-start.1
  3.1 0.9 copy-start.3
  4.0 0.8 copy-start.4
  4.8 0.8 copy-start.5
  5.6 0.8 copy-start.6
where the time goes:
time: 101 us
  Pallas kernels  91.4 us (90%)
  local copies, waits for them, and re-layouts  7.93 us (8%)
    pallas_call x1, Pallas kernels, per_device(): pl.pallas_call(functools.partial(body, groups, ranks), out_shape=(jax.Sha...  91.4 us
    unnamed x27, local copies, waits for them, and re-layouts  6.45 us

commit v1 on v0

v1 whole, which is shorter than its diff:
```python
import functools

import jax
import jax.numpy as jnp
from jax import lax
from jax.experimental import pallas as pl
from jax.experimental.pallas import tpu as pltpu
from jax.sharding import PartitionSpec as P

LANES = 128
SUB = 8
SPAN = 256
MESH = pl.DeviceIdType.MESH

ENDS, PARAMS, STATUS, MULT, DELTA, PIECE, BASE, NET, WORK, ANG, COMP, ENDS2, PARAMS2, SQ, MIS, DUAL, LIM, TOTAL = range(18)
KINDS = 18


def sin_cos(x):
    y = x * x
    sin_c = (1 / 6227020800, -1 / 39916800, 1 / 362880, -1 / 5040, 1 / 120, -1 / 6)
    cos_c = (-1 / 87178291200, 1 / 479001600, -1 / 3628800, 1 / 40320, -1 / 720, 1 / 24, -0.5)
    s = jnp.full_like(y, sin_c[0])
    for c in sin_c[1:]:
        s = s * y + c
    k = jnp.full_like(y, cos_c[0])
    for c in cos_c[1:]:
        k = k * y + c
    return x + x * y * s, 1.0 + y * k


def body(
    groups, ranks,
    vm_any, va_any, delta_any, mult_any, net_any, ang_any, from_any, to_any,
    g_any, b_any, h_any, rating_any, status_any, slack_any, zdual_any,
    mis_out, dual_out, lim_out, norm_out, tot_out,
    vm1, va1, dstg, mstg, nstg, ang8, st8, sl8, zd8, rate,
    ststg, wstg, astg, cstg,
    ebuf, pbuf, stbuf, mbuf, dbuf, zbuf, cbuf, nbuf, wbuf, abuf, compbuf,
    table, dends, dpar, dst, dwork, dlim, acc,
    mout, dout, lout, min_, din, lin, sqbuf, rowbuf,
    local, send, recv,
):
    grp, me = lax.axis_index("ctg"), lax.axis_index("br")
    core = lax.rem(grp, 2)
    sibling = grp + 1 - 2 * core
    scen, _, nb = delta_any.shape
    rows = from_any.shape[0]
    btiles = nb // LANES
    tiles = table.shape[1]
    f32, bf16 = jnp.float32, jnp.bfloat16
    piece_len = vm_any.shape[1]

    def fetch(i, src, dst):
        copy = pltpu.make_async_copy(src, dst, local.at[i])
        copy.start()
        return copy

    ends_in = [pltpu.make_async_copy(src, ebuf.at[me, i], local.at[2 + i]) for i, src in enumerate((from_any, to_any))]
    params_in = [pltpu.make_async_copy(src, pbuf.at[me, i], local.at[8 + i]) for i, src in enumerate((g_any, b_any, h_any))]

    @pl.when(core == 0)
    def _():
        for copy in ends_in:
            copy.start()

    @pl.when(core == 1)
    def _():
        for copy in params_in:
            copy.start()

    base_in = [fetch(0, vm_any, vm1), fetch(1, va_any, va1)]
    status_in = [fetch(4, status_any, st8), fetch(5, slack_any, sl8), fetch(6, zdual_any, zd8), fetch(7, rating_any, rate)]
    bus_in = [fetch(11, delta_any, dstg), fetch(12, mult_any, mstg)]
    late_in = [fetch(13, net_any, nstg), fetch(14, ang_any, ang8)]

    barrier = pltpu.get_barrier_semaphore()

    def greet_near(i, carry):
        pl.semaphore_signal(barrier, inc=1, device_id=(grp, lax.rem(me + i, ranks)), device_id_type=MESH)
        return carry

    def greet_far(i, carry):
        pl.semaphore_signal(barrier, inc=1, device_id=(lax.rem(grp + i, groups), me), device_id_type=MESH)
        return carry

    lax.fori_loop(1, ranks, greet_near, 0)
    lax.fori_loop(1, groups, greet_far, 0)

    for copy in base_in + status_in:
        copy.wait()

    lane = lax.broadcasted_iota(jnp.int32, (SUB, LANES), 1)
    pad = jnp.zeros((1, LANES - piece_len), f32)
    piece = jnp.concatenate(
        [jnp.concatenate([vm1[...], pad], axis=1), jnp.concatenate([va1[...], pad], axis=1), jnp.zeros((SUB - 2, LANES), f32)],
        axis=0,
    )
    shift = lax.rem(grp * (ranks * piece_len) + me * piece_len, LANES)
    piece = pltpu.roll(piece, shift, 1)
    zbuf[me] = piece[0:2, :]

    for r in range(rows):
        cols = slice(r * LANES, (r + 1) * LANES)
        ststg[:, r, :] = st8[:, cols]
        wstg[:, r, :] = sl8[:, cols]
    squared = rate[...] * rate[...]
    for s in range(scen):
        wstg[s] = wstg[s] - squared
    comp = st8[...].astype(f32) * (zd8[...] * sl8[...] - 0.01)
    cstg[:, 0, :] = jnp.broadcast_to(jnp.sum(comp * comp, axis=1, keepdims=True), (scen, LANES))

    for copy in bus_in + late_in:
        copy.wait()
    for k in range(btiles):
        astg[:, k, :] = ang8[:, k * LANES : (k + 1) * LANES]

    pl.semaphore_wait(barrier, ranks - 1 + groups - 1)

    def near(kind, step, src, dst):
        pltpu.make_async_remote_copy(
            src_ref=src, dst_ref=dst, send_sem=send.at[kind], recv_sem=recv.at[kind],
            device_id=(grp, lax.rem(me + step, ranks)), device_id_type=MESH,
        ).start()

    def far(kind, step, src, dst):
        pltpu.make_async_remote_copy(
            src_ref=src, dst_ref=dst, send_sem=send.at[kind], recv_sem=recv.at[kind],
            device_id=(lax.rem(grp + step, groups), me), device_id_type=MESH,
        ).start()

    def across(kind, ref):
        return pltpu.make_async_remote_copy(
            src_ref=ref, dst_ref=ref, send_sem=send.at[kind], recv_sem=recv.at[kind],
            device_id=(sibling, me), device_id_type=MESH,
        )

    def whole(kind, ref, n):
        part = ref.at[pl.ds(0, n)]
        return pltpu.make_async_remote_copy(
            src_ref=part, dst_ref=part, send_sem=send.at[kind], recv_sem=recv.at[kind],
            device_id=(sibling, me), device_id_type=MESH,
        )

    def to_near(kind, src_of, dst):
        def go(step, carry):
            near(kind, step, src_of(lax.rem(me + step, ranks)), dst)
            return carry
        lax.fori_loop(1, ranks, go, 0)

    def to_far(kind, src, dst):
        def go(step, carry):
            far(kind, step, src, dst)
            return carry
        lax.fori_loop(1, groups, go, 0)

    to_near(PIECE, lambda p: zbuf.at[me], zbuf.at[me])

    @pl.when(core == 0)
    def _():
        for copy in ends_in:
            copy.wait()
        to_near(ENDS, lambda p: ebuf.at[me], ebuf.at[me])

    @pl.when(core == 1)
    def _():
        for copy in params_in:
            copy.wait()
        to_near(PARAMS, lambda p: pbuf.at[me], pbuf.at[me])

    to_near(STATUS, lambda p: ststg.at[p], stbuf.at[me])
    to_near(DELTA, lambda p: dstg.at[p], dbuf.at[me])
    to_near(MULT, lambda p: mstg.at[p], mbuf.at[me])
    to_near(COMP, lambda p: cstg.at[p], compbuf.at[me])
    to_near(NET, lambda p: nstg.at[p], nbuf.at[me])
    to_near(WORK, lambda p: wstg.at[p], wbuf.at[me])
    to_near(ANG, lambda p: astg.at[p], abuf.at[me])

    stbuf[me] = ststg[me]
    dbuf[me] = dstg[me]
    mbuf[me] = mstg[me]
    nbuf[me] = nstg[me]
    wbuf[me] = wstg[me]
    abuf[me] = astg[me]
    compbuf[me] = cstg[me]
    acc[...] = jnp.zeros_like(acc)

    whole(PIECE, zbuf, ranks - 1).wait_recv()
    window = (LANES // 2) * core
    for m in range(3):
        off = m * LANES + lane[0:2, :] - window
        found = jnp.zeros((2, LANES), f32)
        for b in range(ranks):
            inside = (off >= b * piece_len) & (off < (b + 1) * piece_len)
            found = jnp.where(inside, zbuf[b], found)
        cbuf[grp, m : m + 1, :] = found[0:1, :]
        cbuf[grp, 3 + m : 4 + m, :] = found[1:2, :]
    cbuf[grp, 6:8, :] = jnp.zeros((2, LANES), f32)
    to_far(BASE, cbuf.at[grp], cbuf.at[grp])

    @pl.when(core == 0)
    def _():
        whole(ENDS, ebuf, ranks - 1).wait_recv()
        across(ENDS2, ebuf).start()

    @pl.when(core == 1)
    def _():
        whole(PARAMS, pbuf, ranks - 1).wait_recv()
        across(PARAMS2, pbuf).start()
        across(ENDS2, ebuf).wait_recv()

    for end in range(2):
        for z in range(ranks):
            dends[end, z * rows : (z + 1) * rows, :] = ebuf[z, end]

    whole(MULT, mbuf, ranks - 1).wait_recv()
    for z in range(ranks):
        for q in range(2):
            for k in range(btiles):
                at = z * btiles + k
                table[2 + q, at : at + 1, :] = mbuf[z, q : q + 1, k * LANES : (k + 1) * LANES]

    whole(STATUS, stbuf, ranks - 1).wait_recv()
    for z in range(ranks):
        dst[z * rows : (z + 1) * rows, :] = stbuf[z]

    @pl.when(core == 0)
    def _():
        across(PARAMS2, pbuf).wait_recv()

    for q in range(3):
        for z in range(ranks):
            dpar[q, z * rows : (z + 1) * rows, :] = pbuf[z, q]

    whole(DELTA, dbuf, ranks - 1).wait_recv()
    whole(BASE, cbuf, groups - 1).wait_recv()
    for r in range(groups // 2):
        for q in range(2):
            def one(c, m):
                return cbuf[2 * r + c, 3 * q + m : 3 * q + m + 1, :]
            five = (one(0, 0), one(0, 1), one(0, 2) + one(1, 0), one(1, 1), one(1, 2))
            for m in range(5):
                at = 5 * r + m
                z, k = at // btiles, at % btiles
                table[q, at : at + 1, :] = five[m] + dbuf[z, q : q + 1, k * LANES : (k + 1) * LANES]

    chunks = dends.shape[1] // SUB
    high = acc.shape[0] // 6
    used = tiles * LANES // SPAN
    label = lax.broadcasted_iota(jnp.int32, (SPAN, LANES), 0).astype(bf16)
    steps = lax.broadcasted_iota(jnp.int32, (high, LANES), 0).astype(bf16)

    def at_rows(i):
        return pl.ds(pl.multiple_of(i * SUB, SUB), SUB)

    def pick(i):
        picked = []
        for end in range(2):
            spot = dends[end, at_rows(i), :]
            low, tile = spot & (LANES - 1), spot >> 7
            found = [jnp.zeros((SUB, LANES), f32) for _ in range(4)]
            for k in range(tiles):
                here = tile == k
                for q in range(4):
                    row = jnp.broadcast_to(table[q, k : k + 1, :], (SUB, LANES))
                    got = jnp.take_along_axis(row, low, axis=1, mode="promise_in_bounds")
                    found[q] = jnp.where(here, got, found[q])
            picked += found
        return tuple(picked)

    def spread(x, n):
        return jnp.concatenate([jnp.broadcast_to(x, (2 * SUB, LANES)).astype(bf16)] * (n // (2 * SUB)), axis=0)

    def process(i, picked):
        vf, af, mpf, mqf, vt, at, mpt, mqt = picked
        where_ = at_rows(i)
        sn, cs = sin_cos(af - at)
        g, b, h = dpar[0, where_, :], dpar[1, where_, :], dpar[2, where_, :]
        live = dst[where_, :].astype(f32)
        u = vf * vt
        gc_bs, gc_mbs = g * cs + b * sn, g * cs - b * sn
        gs_bc, gs_mbc = g * sn + b * cs, g * sn - b * cs
        bh = -(b + h)
        pf = live * (g * vf * vf - u * gc_bs)
        qf = live * (bh * vf * vf - u * gs_mbc)
        pt = live * (g * vt * vt - u * gc_mbs)
        qt = live * (bh * vt * vt + u * gs_bc)
        fd = live * u * (mpf * gs_mbc - mqf * gc_bs + mpt * gs_bc + mqt * gc_mbs)
        dlim[where_, :] = pf * pf + qf * qf
        total = None
        for end, terms in ((0, (pf, qf, fd)), (1, (pt, qt, -fd))):
            parts = []
            for value in terms:
                head = value.astype(bf16).astype(f32)
                parts += [head, value - head]
            spot = dends[end, where_, :]
            low, tile = spot & (SPAN - 1), spot >> 8
            lefts, hots = [], []
            for r in range(SUB):
                row = slice(r, r + 1)
                mask = spread(tile[row, :], high) == steps
                lefts.append(jnp.concatenate(
                    [jnp.where(mask, spread(x[row, :], high), bf16(0)) for x in parts], axis=0
                ))
                hots.append(jnp.where(spread(low[row, :], SPAN) == label, bf16(1), bf16(0)))
            dot = lax.dot_general(
                jnp.concatenate(lefts, axis=1), jnp.concatenate(hots, axis=1),
                (((1,), (1,)), ((), ())), preferred_element_type=f32,
            )
            total = dot if total is None else total + dot
        acc[...] += total

    def advance(i, picked):
        following = pick(i + 1)
        process(i, picked)
        return following

    process(chunks - 1, lax.fori_loop(0, chunks - 1, advance, pick(0)))

    whole(NET, nbuf, ranks - 1).wait_recv()
    whole(WORK, wbuf, ranks - 1).wait_recv()
    whole(ANG, abuf, ranks - 1).wait_recv()
    whole(COMP, compbuf, ranks - 1).wait_recv()

    per = nb // SPAN
    mis_sq = jnp.zeros((1, SPAN), f32)
    dual_sq = jnp.zeros((1, LANES), f32)
    for z in range(ranks):
        for j in range(per):
            t = z * per + j
            cols = slice(j * SPAN, (j + 1) * SPAN)
            for q in range(3):
                top, bottom = (2 * q) * high + t, (2 * q + 1) * high + t
                row = acc[top : top + 1, :] + acc[bottom : bottom + 1, :]
                if q < 2:
                    row = row - nbuf[z, q : q + 1, cols]
                    mout[z, q : q + 1, cols] = row
                    mis_sq = mis_sq + row * row
                else:
                    for half in range(2):
                        k = 2 * j + half
                        one = row[:, half * LANES : (half + 1) * LANES] + abuf[z, k : k + 1, :]
                        dout[z, k : k + 1, :] = one
                        dual_sq = dual_sq + one * one
    lim_sq = jnp.zeros((rows, LANES), f32)
    for z in range(ranks):
        lim = stbuf[z].astype(f32) * (dlim[z * rows : (z + 1) * rows, :] + wbuf[z])
        lout[z] = lim
        lim_sq = lim_sq + lim * lim
    comp_sq = jnp.zeros((1, LANES), f32)
    for z in range(ranks):
        comp_sq = comp_sq + compbuf[z]

    def total_of(x):
        return jnp.sum(jnp.sum(x, axis=0, keepdims=True), axis=1, keepdims=True)

    lane1 = lane[0:1, :]
    squares = jnp.where(
        lane1 == 0, total_of(mis_sq),
        jnp.where(lane1 == 1, total_of(dual_sq), jnp.where(lane1 == 2, total_of(lim_sq), jnp.where(lane1 == 3, comp_sq, 0.0))),
    )
    sqbuf[me] = squares
    to_near(SQ, lambda p: sqbuf.at[me], sqbuf.at[me])
    to_near(MIS, lambda p: mout.at[p], min_.at[me])
    to_near(DUAL, lambda p: dout.at[p], din.at[me])
    to_near(LIM, lambda p: lout.at[p], lin.at[me])
    min_[me] = mout[me]
    din[me] = dout[me]
    lin[me] = lout[me]

    whole(SQ, sqbuf, ranks - 1).wait_recv()
    column = jnp.zeros((1, LANES), f32)
    for z in range(ranks):
        one = sqbuf[z]
        column = column + one
        norm_out[z : z + 1, :] = jnp.sqrt(one[:, 0:4])
    rowbuf[grp] = column
    to_far(TOTAL, rowbuf.at[grp], rowbuf.at[grp])

    whole(MIS, min_, ranks - 1).wait_recv()
    mis_out[...] = min_[...]
    whole(DUAL, din, ranks - 1).wait_recv()
    for k in range(btiles):
        dual_out[:, k * LANES : (k + 1) * LANES] = din[:, k, :]
    whole(LIM, lin, ranks - 1).wait_recv()
    for r in range(rows):
        lim_out[:, r * LANES : (r + 1) * LANES] = lin[:, r, :]

    @pl.when(core == 0)
    def _():
        whole(ENDS, ebuf, ranks - 1).wait_send()
        across(ENDS2, ebuf).wait_send()

    @pl.when(core == 1)
    def _():
        whole(PARAMS, pbuf, ranks - 1).wait_send()
        across(PARAMS2, pbuf).wait_send()

    for kind, ref in (
        (PIECE, zbuf), (STATUS, ststg), (DELTA, dstg), (MULT, mstg), (COMP, cstg), (NET, nstg), (WORK, wstg),
        (ANG, astg), (SQ, sqbuf), (MIS, mout), (DUAL, dout), (LIM, lout),
    ):
        whole(kind, ref, ranks - 1).wait_send()
    whole(BASE, cbuf, groups - 1).wait_send()
    whole(TOTAL, rowbuf, groups - 1).wait_send()

    whole(TOTAL, rowbuf, groups - 1).wait_recv()
    everything = jnp.zeros((1, LANES), f32)
    for i in range(groups):
        everything = everything + rowbuf[i]
    tot_out[...] = jnp.sqrt(everything[:, 0:4] / (scen * groups))


def per_device(
    base_vm, base_va, delta_state, multipliers, net_inj, ang_grad, from_bus, to_bus,
    status, conduct, suscept, charging, rating, slack, zdual,
):
    groups, ranks = lax.axis_size("ctg"), lax.axis_size("br")
    scen, _, nb = delta_state.shape
    nl = from_bus.shape[0]
    rows, btiles = nl // LANES, nb // LANES
    buses = nb * ranks
    tiles = buses // LANES
    high = -(-(buses // SPAN) // 16) * 16
    block = base_vm.shape[0]
    f32, i32 = jnp.float32, jnp.int32
    vmem = pl.BlockSpec(memory_space=pltpu.VMEM)
    hbm = pl.BlockSpec(memory_space=pltpu.HBM)
    V = pltpu.VMEM
    mis, dual, lim, norms, tot = pl.pallas_call(
        functools.partial(body, groups, ranks),
        out_shape=(
            jax.ShapeDtypeStruct((scen, 2, nb), f32),
            jax.ShapeDtypeStruct((scen, nb), f32),
            jax.ShapeDtypeStruct((scen, nl), f32),
            jax.ShapeDtypeStruct((scen, 4), f32),
            jax.ShapeDtypeStruct((1, 4), f32),
        ),
        in_specs=[hbm] * 15,
        out_specs=(vmem,) * 5,
        scratch_shapes=[
            V((1, block), f32), V((1, block), f32),
            V((scen, 2, nb), f32), V((scen, 2, nb), f32), V((scen, 2, nb), f32),
            V((scen, nb), f32), V((scen, nl), i32), V((scen, nl), f32), V((scen, nl), f32), V((rows, LANES), f32),
            V((scen, rows, LANES), i32), V((scen, rows, LANES), f32), V((scen, btiles, LANES), f32), V((scen, 1, LANES), f32),
            V((ranks, 2, rows, LANES), i32), V((ranks, 3, rows, LANES), f32), V((ranks, rows, LANES), i32),
            V((ranks, 2, nb), f32), V((ranks, 2, nb), f32), V((ranks, 2, LANES), f32), V((groups, SUB, LANES), f32),
            V((ranks, 2, nb), f32), V((ranks, rows, LANES), f32), V((ranks, btiles, LANES), f32), V((ranks, 1, LANES), f32),
            V((4, tiles, LANES), f32), V((2, ranks * rows, LANES), i32), V((3, ranks * rows, LANES), f32),
            V((ranks * rows, LANES), i32), V((ranks * rows, LANES), f32), V((ranks * rows, LANES), f32), V((6 * high, SPAN), f32),
            V((ranks, 2, nb), f32), V((ranks, btiles, LANES), f32), V((ranks, rows, LANES), f32),
            V((ranks, 2, nb), f32), V((ranks, btiles, LANES), f32), V((ranks, rows, LANES), f32),
            V((ranks, 1, LANES), f32), V((groups, 1, LANES), f32),
            pltpu.SemaphoreType.DMA((15,)),
            pltpu.SemaphoreType.DMA((KINDS,)),
            pltpu.SemaphoreType.DMA((KINDS,)),
        ],
        compiler_params=pltpu.CompilerParams(
            collective_id=0, has_side_effects=True, vmem_limit_bytes=40 << 20
        ),
    )(*(pltpu.with_memory_space_constraint(x, pltpu.HBM) for x in (
        base_vm[None, :], base_va[None, :], delta_state, multipliers, net_inj, ang_grad,
        *(x.reshape(rows, LANES) for x in (from_bus, to_bus, conduct, suscept, charging, rating)),
        status, slack, zdual,
    )))
    return (mis, dual, lim, norms, tot[0])


def solution(mesh):
    placed = (
        P(("ctg", "br")), P(("ctg", "br")),
        P("ctg", None, "br"), P("ctg", None, "br"), P("ctg", None, "br"), P("ctg", "br"),
        P("br"), P("br"), P("ctg", "br"), P("br"), P("br"), P("br"), P("br"),
        P("ctg", "br"), P("ctg", "br"),
    )
    return jax.shard_map(
        per_device,
        mesh=mesh,
        in_specs=placed,
        out_specs=(P("ctg", None, "br"), P("ctg", "br"), P("ctg", "br"), P("ctg", None), P()),
        check_vma=False,
    )
```

time: 101 us -> 47.4 us (0.47)
  Pallas kernels: 91.4 us -> 43.6 us
  local copies, waits for them, and re-layouts: 7.93 us -> 3.04 us
    pallas_call x1, Pallas kernels: 91.4 us -> 43.6 us  [per_device(): pl.pallas_call(functools.partial(body, groups, ranks), out_shape=(jax.Sha...]
    unnamed x27 -> x5, local copies, waits for them, and re-layouts: 6.45 us -> 3.04 us
where the time goes in v1:
time: 47.4 us; the launch traced here: 47.3 us
  Pallas kernels  43.6 us (92%)
  local copies, waits for them, and re-layouts  3.04 us (6%)
  between operations  0.65 us (1%)
    pallas_call x1, Pallas kernels, per_device(): pl.pallas_call(functools.partial(body, groups, ranks), out_shape=(jax.Sha...  43.6 us
    unnamed x5, local copies, waits for them, and re-layouts  3.04 us

profile of v1, /device:TPU:1, one launch (start us, length us, event | category | flops | bytes accessed | tf_op | source)
XLA Modules:
  0.0 47.3 jit_solution(12173736018826707418)
XLA Ops:
  0.6 43.6 %shard_map.182 = (f32[8,2,1280]{2,1,0:T(2,128)S(1)}, f32[8,1280]{1,0:T(8,128)S(1)}, f32[8,1664]{1,0:T(8,128)S(1)}, f32[8,4]{1,0:T(8,128)S(1)}, f32[1,4]{1,0:T(1,128)S(1)}) custom-call(f32[1,40]{1,0:T(1,128)} %bitcast.16, f32[1,40]{1,0:T(1,128)} %bitcast.17, f32[8,2,1280]{2,1,0:T(2,128)} %delta_any.1, f32[8,2,1280]{2,1,0:T(2,128)} %mult_any.1, ...), custom_call_target="tpu_custom_call" | custom-call | tf_op jit(solution)/shard_map/pallas_call | solution.py:430
  44.2 0.7 %copy.20 = f32[8,4]{0,1:T(4,128)} copy(f32[8,4]{1,0:T(8,128)S(1)} %get-tuple-element.18) | data formatting | bytes 256
  44.9 0.6 %copy.25 = f32[8,2,1280]{2,1,0:T(2,128)} copy(f32[8,2,1280]{2,1,0:T(2,128)S(1)} %get-tuple-element.25) | data formatting | bytes 163840
  45.5 0.6 %copy.26 = f32[8,1280]{1,0:T(8,128)} copy(f32[8,1280]{1,0:T(8,128)S(1)} %get-tuple-element.26) | data formatting | bytes 81920
  46.1 0.6 %copy.27 = f32[8,1664]{1,0:T(8,128)} copy(f32[8,1664]{1,0:T(8,128)S(1)} %get-tuple-element.27) | data formatting | bytes 106496
  46.8 0.5 %copy.28 = f32[4]{0:T(128)} copy(f32[4]{0:T(128)S(1)} %bitcast.9) | data formatting | bytes 32

commit v2 on v1

--- a/solution.py
+++ b/solution.py
@@ -33,12 +33,12 @@
     groups, ranks,
     vm_any, va_any, delta_any, mult_any, net_any, ang_any, from_any, to_any,
     g_any, b_any, h_any, rating_any, status_any, slack_any, zdual_any,
-    mis_out, dual_out, lim_out, norm_out, tot_out,
+    min_, din, lin, norm_out, tot_out,
     vm1, va1, dstg, mstg, nstg, ang8, st8, sl8, zd8, rate,
     ststg, wstg, astg, cstg,
-    ebuf, pbuf, stbuf, mbuf, dbuf, zbuf, cbuf, nbuf, wbuf, abuf, compbuf,
-    table, dends, dpar, dst, dwork, dlim, acc,
-    mout, dout, lout, min_, din, lin, sqbuf, rowbuf,
+    ebuf, pbuf0, pbuf1, stbuf, mbuf, dbuf, zbuf, cbuf, nbuf, wbuf, abuf, compbuf,
+    table, dends, dpar, dst, dmult, dlim, hot, acc,
+    mout, dout, lout, sqbuf, rowbuf,
     local, send, recv,
 ):
     grp, me = lax.axis_index("ctg"), lax.axis_index("br")
@@ -56,17 +56,20 @@
         copy.start()
         return copy
 
-    ends_in = [pltpu.make_async_copy(src, ebuf.at[me, i], local.at[2 + i]) for i, src in enumerate((from_any, to_any))]
-    params_in = [pltpu.make_async_copy(src, pbuf.at[me, i], local.at[8 + i]) for i, src in enumerate((g_any, b_any, h_any))]
+    ends_in = [pltpu.make_async_copy(src, ebuf.at[i, me], local.at[2 + i]) for i, src in enumerate((from_any, to_any))]
+    params_in = [
+        pltpu.make_async_copy(src, dst, local.at[8 + i])
+        for i, (src, dst) in enumerate(((g_any, pbuf0.at[me, 0]), (h_any, pbuf0.at[me, 1]), (b_any, pbuf1.at[me, 0])))
+    ]
 
     @pl.when(core == 0)
     def _():
-        for copy in ends_in:
+        for copy in (ends_in[0], params_in[0], params_in[1]):
             copy.start()
 
     @pl.when(core == 1)
     def _():
-        for copy in params_in:
+        for copy in (ends_in[1], params_in[2]):
             copy.start()
 
     base_in = [fetch(0, vm_any, vm1), fetch(1, va_any, va1)]
@@ -158,19 +161,29 @@
 
     @pl.when(core == 0)
     def _():
-        for copy in ends_in:
-            copy.wait()
-        to_near(ENDS, lambda p: ebuf.at[me], ebuf.at[me])
+        ends_in[0].wait()
+        to_near(ENDS, lambda p: ebuf.at[0, me], ebuf.at[0, me])
 
     @pl.when(core == 1)
     def _():
-        for copy in params_in:
-            copy.wait()
-        to_near(PARAMS, lambda p: pbuf.at[me], pbuf.at[me])
-
+        ends_in[1].wait()
+        to_near(ENDS, lambda p: ebuf.at[1, me], ebuf.at[1, me])
+
+    to_near(MULT, lambda p: mstg.at[p], mbuf.at[me])
+    to_near(DELTA, lambda p: dstg.at[p], dbuf.at[me])
     to_near(STATUS, lambda p: ststg.at[p], stbuf.at[me])
-    to_near(DELTA, lambda p: dstg.at[p], dbuf.at[me])
-    to_near(MULT, lambda p: mstg.at[p], mbuf.at[me])
+
+    @pl.when(core == 0)
+    def _():
+        params_in[0].wait()
+        params_in[1].wait()
+        to_near(PARAMS, lambda p: pbuf0.at[me], pbuf0.at[me])
+
+    @pl.when(core == 1)
+    def _():
+        params_in[2].wait()
+        to_near(PARAMS, lambda p: pbuf1.at[me], pbuf1.at[me])
+
     to_near(COMP, lambda p: cstg.at[p], compbuf.at[me])
     to_near(NET, lambda p: nstg.at[p], nbuf.at[me])
     to_near(WORK, lambda p: wstg.at[p], wbuf.at[me])
@@ -198,20 +211,39 @@
     cbuf[grp, 6:8, :] = jnp.zeros((2, LANES), f32)
     to_far(BASE, cbuf.at[grp], cbuf.at[grp])
 
-    @pl.when(core == 0)
-    def _():
-        whole(ENDS, ebuf, ranks - 1).wait_recv()
-        across(ENDS2, ebuf).start()
-
-    @pl.when(core == 1)
-    def _():
-        whole(PARAMS, pbuf, ranks - 1).wait_recv()
-        across(PARAMS2, pbuf).start()
-        across(ENDS2, ebuf).wait_recv()
+    for c in range(2):
+        @pl.when(core == c)
+        def _(c=c):
+            whole(ENDS, ebuf.at[c], ranks - 1).wait_recv()
+            across(ENDS2, ebuf.at[c]).start()
+            across(ENDS2, ebuf.at[1 - c]).wait_recv()
 
     for end in range(2):
         for z in range(ranks):
-            dends[end, z * rows : (z + 1) * rows, :] = ebuf[z, end]
+            dends[end, z * rows : (z + 1) * rows, :] = ebuf[end, z]
+
+    chunks = dends.shape[1] // SUB
+    high = acc.shape[0] // 6
+    column0 = lax.broadcasted_iota(jnp.int32, (LANES, LANES), 1)
+    labels = [(column0 + k * LANES).astype(bf16) for k in range(SPAN // LANES)]
+    steps = lax.broadcasted_iota(jnp.int32, (high, LANES), 0).astype(bf16)
+
+    def at_rows(i):
+        return pl.ds(pl.multiple_of(i * SUB, SUB), SUB)
+
+    def spread(x, n):
+        return jnp.concatenate([jnp.broadcast_to(x, (2 * SUB, LANES)).astype(bf16)] * (n // (2 * SUB)), axis=0)
+
+    def make_hot(i, carry):
+        for end in range(2):
+            low = dends[end, at_rows(i), :] & (SPAN - 1)
+            for r in range(SUB):
+                spots = spread(low[r : r + 1, :], LANES).T
+                for k, label in enumerate(labels):
+                    hot[end, i, k, r * LANES : (r + 1) * LANES, :] = jnp.where(spots == label, bf16(1), bf16(0))
+        return carry
+
+    lax.fori_loop(0, chunks, make_hot, 0)
 
     whole(MULT, mbuf, ranks - 1).wait_recv()
     for z in range(ranks):
@@ -220,20 +252,58 @@
                 at = z * btiles + k
                 table[2 + q, at : at + 1, :] = mbuf[z, q : q + 1, k * LANES : (k + 1) * LANES]
 
+    def pick(i, first):
+        picked = []
+        for end in range(2):
+            spot = dends[end, at_rows(i), :]
+            low, tile = spot & (LANES - 1), spot >> 7
+            found = [jnp.zeros((SUB, LANES), f32) for _ in range(2)]
+            for k in range(tiles):
+                here = tile == k
+                for q in range(2):
+                    row = jnp.broadcast_to(table[first + q, k : k + 1, :], (SUB, LANES))
+                    got = jnp.take_along_axis(row, low, axis=1, mode="promise_in_bounds")
+                    found[q] = jnp.where(here, got, found[q])
+            picked += found
+        return tuple(picked)
+
+    def keep(i):
+        for k, x in enumerate(pick(i, 2)):
+            dmult[k, at_rows(i), :] = x
+
+    def keep_two(j, carry):
+        keep(2 * j)
+        keep(2 * j + 1)
+        return carry
+
+    lax.fori_loop(0, chunks // 2, keep_two, 0)
+    if chunks % 2:
+        keep(chunks - 1)
+
     whole(STATUS, stbuf, ranks - 1).wait_recv()
     for z in range(ranks):
         dst[z * rows : (z + 1) * rows, :] = stbuf[z]
 
     @pl.when(core == 0)
     def _():
-        across(PARAMS2, pbuf).wait_recv()
-
-    for q in range(3):
-        for z in range(ranks):
-            dpar[q, z * rows : (z + 1) * rows, :] = pbuf[z, q]
+        whole(PARAMS, pbuf0, ranks - 1).wait_recv()
+        across(PARAMS2, pbuf0).start()
+        across(PARAMS2, pbuf1).wait_recv()
+
+    @pl.when(core == 1)
+    def _():
+        whole(PARAMS, pbuf1, ranks - 1).wait_recv()
+        across(PARAMS2, pbuf1).start()
+        across(PARAMS2, pbuf0).wait_recv()
+
+    for z in range(ranks):
+        dpar[0, z * rows : (z + 1) * rows, :] = pbuf0[z, 0]
+        dpar[1, z * rows : (z + 1) * rows, :] = pbuf1[z, 0]
+        dpar[2, z * rows : (z + 1) * rows, :] = pbuf0[z, 1]
 
     whole(DELTA, dbuf, ranks - 1).wait_recv()
     whole(BASE, cbuf, groups - 1).wait_recv()
+
     for r in range(groups // 2):
         for q in range(2):
             def one(c, m):
@@ -244,36 +314,10 @@
                 z, k = at // btiles, at % btiles
                 table[q, at : at + 1, :] = five[m] + dbuf[z, q : q + 1, k * LANES : (k + 1) * LANES]
 
-    chunks = dends.shape[1] // SUB
-    high = acc.shape[0] // 6
-    used = tiles * LANES // SPAN
-    label = lax.broadcasted_iota(jnp.int32, (SPAN, LANES), 0).astype(bf16)
-    steps = lax.broadcasted_iota(jnp.int32, (high, LANES), 0).astype(bf16)
-
-    def at_rows(i):
-        return pl.ds(pl.multiple_of(i * SUB, SUB), SUB)
-
-    def pick(i):
-        picked = []
-        for end in range(2):
-            spot = dends[end, at_rows(i), :]
-            low, tile = spot & (LANES - 1), spot >> 7
-            found = [jnp.zeros((SUB, LANES), f32) for _ in range(4)]
-            for k in range(tiles):
-                here = tile == k
-                for q in range(4):
-                    row = jnp.broadcast_to(table[q, k : k + 1, :], (SUB, LANES))
-                    got = jnp.take_along_axis(row, low, axis=1, mode="promise_in_bounds")
-                    found[q] = jnp.where(here, got, found[q])
-            picked += found
-        return tuple(picked)
-
-    def spread(x, n):
-        return jnp.concatenate([jnp.broadcast_to(x, (2 * SUB, LANES)).astype(bf16)] * (n // (2 * SUB)), axis=0)
-
-    def process(i, picked):
-        vf, af, mpf, mqf, vt, at, mpt, mqt = picked
+    def scatter(i, picked):
+        vf, af, vt, at = picked
         where_ = at_rows(i)
+        mpf, mqf, mpt, mqt = (dmult[k, where_, :] for k in range(4))
         sn, cs = sin_cos(af - at)
         g, b, h = dpar[0, where_, :], dpar[1, where_, :], dpar[2, where_, :]
         live = dst[where_, :].astype(f32)
@@ -293,29 +337,36 @@
             for value in terms:
                 head = value.astype(bf16).astype(f32)
                 parts += [head, value - head]
-            spot = dends[end, where_, :]
-            low, tile = spot & (SPAN - 1), spot >> 8
-            lefts, hots = [], []
+            tile = dends[end, where_, :] >> 8
+            lefts = []
             for r in range(SUB):
                 row = slice(r, r + 1)
                 mask = spread(tile[row, :], high) == steps
                 lefts.append(jnp.concatenate(
                     [jnp.where(mask, spread(x[row, :], high), bf16(0)) for x in parts], axis=0
                 ))
-                hots.append(jnp.where(spread(low[row, :], SPAN) == label, bf16(1), bf16(0)))
+            right = jnp.concatenate([hot[end, i, k] for k in range(SPAN // LANES)], axis=1)
             dot = lax.dot_general(
-                jnp.concatenate(lefts, axis=1), jnp.concatenate(hots, axis=1),
-                (((1,), (1,)), ((), ())), preferred_element_type=f32,
+                jnp.concatenate(lefts, axis=1), right, (((1,), (0,)), ((), ())), preferred_element_type=f32
             )
             total = dot if total is None else total + dot
-        acc[...] += total
-
-    def advance(i, picked):
-        following = pick(i + 1)
-        process(i, picked)
+        return total
+
+    def two(i):
+        return pick(i, 0) + pick(i + 1, 0)
+
+    def scatter_two(i, picked):
+        acc[...] += scatter(i, picked[:4]) + scatter(i + 1, picked[4:])
+
+    def advance(j, picked):
+        following = two(2 * j + 1)
+        scatter_two(2 * j - 1, picked)
         return following
 
-    process(chunks - 1, lax.fori_loop(0, chunks - 1, advance, pick(0)))
+    first = pick(0, 0)
+    following = two(1)
+    acc[...] += scatter(0, first)
+    scatter_two(chunks - 2, lax.fori_loop(1, chunks // 2, advance, following))
 
     whole(NET, nbuf, ranks - 1).wait_recv()
     whole(WORK, wbuf, ranks - 1).wait_recv()
@@ -373,28 +424,26 @@
     for z in range(ranks):
         one = sqbuf[z]
         column = column + one
-        norm_out[z : z + 1, :] = jnp.sqrt(one[:, 0:4])
+        norm_out[z : z + 1, :] = jnp.sqrt(one)
     rowbuf[grp] = column
     to_far(TOTAL, rowbuf.at[grp], rowbuf.at[grp])
 
     whole(MIS, min_, ranks - 1).wait_recv()
-    mis_out[...] = min_[...]
     whole(DUAL, din, ranks - 1).wait_recv()
-    for k in range(btiles):
-        dual_out[:, k * LANES : (k + 1) * LANES] = din[:, k, :]
     whole(LIM, lin, ranks - 1).wait_recv()
-    for r in range(rows):
-        lim_out[:, r * LANES : (r + 1) * LANES] = lin[:, r, :]
+
+    whole(ENDS, ebuf.at[0], ranks - 1).wait_send()
+    across(ENDS2, ebuf.at[0]).wait_send()
 
     @pl.when(core == 0)
     def _():
-        whole(ENDS, ebuf, ranks - 1).wait_send()
-        across(ENDS2, ebuf).wait_send()
+        whole(PARAMS, pbuf0, ranks - 1).wait_send()
+        across(PARAMS2, pbuf0).wait_send()
 
     @pl.when(core == 1)
     def _():
-        whole(PARAMS, pbuf, ranks - 1).wait_send()
-        across(PARAMS2, pbuf).wait_send()
+        whole(PARAMS, pbuf1, ranks - 1).wait_send()
+        across(PARAMS2, pbuf1).wait_send()
 
     for kind, ref in (
         (PIECE, zbuf), (STATUS, ststg), (DELTA, dstg), (MULT, mstg), (COMP, cstg), (NET, nstg), (WORK, wstg),
@@ -409,6 +458,27 @@
     for i in range(groups):
         everything = everything + rowbuf[i]
     tot_out[...] = jnp.sqrt(everything[:, 0:4] / (scen * groups))
+
+
+def write_out(min_, din, lin, norms, tot, mis_any, dual_any, lim_any, norm_any, tot_any, dual, lim, turned, sems):
+    copies = [
+        pltpu.make_async_copy(src, dst, sems.at[i])
+        for i, (src, dst) in enumerate((
+            (min_, mis_any), (tot, tot_any), (dual, dual_any), (lim, lim_any), (turned, norm_any),
+        ))
+    ]
+    copies[0].start()
+    copies[1].start()
+    for k in range(din.shape[1]):
+        dual[:, k * LANES : (k + 1) * LANES] = din[:, k, :]
+    copies[2].start()
+    for r in range(lin.shape[1]):
+        lim[:, r * LANES : (r + 1) * LANES] = lin[:, r, :]
+    copies[3].start()
+    turned[...] = norms[...].T[0:4, :]
+    copies[4].start()
+    for copy in copies:
+        copy.wait()
 
 
 def per_device(
@@ -427,13 +497,13 @@
     vmem = pl.BlockSpec(memory_space=pltpu.VMEM)
     hbm = pl.BlockSpec(memory_space=pltpu.HBM)
     V = pltpu.VMEM
-    mis, dual, lim, norms, tot = pl.pallas_call(
+    outs = pl.pallas_call(
         functools.partial(body, groups, ranks),
         out_shape=(
-            jax.ShapeDtypeStruct((scen, 2, nb), f32),
-            jax.ShapeDtypeStruct((scen, nb), f32),
-            jax.ShapeDtypeStruct((scen, nl), f32),
-            jax.ShapeDtypeStruct((scen, 4), f32),
+            jax.ShapeDtypeStruct((ranks, 2, nb), f32),
+            jax.ShapeDtypeStruct((ranks, btiles, LANES), f32),
+            jax.ShapeDtypeStruct((ranks, rows, LANES), f32),
+            jax.ShapeDtypeStruct((scen, LANES), f32),
             jax.ShapeDtypeStruct((1, 4), f32),
         ),
         in_specs=[hbm] * 15,
@@ -443,12 +513,13 @@
             V((scen, 2, nb), f32), V((scen, 2, nb), f32), V((scen, 2, nb), f32),
             V((scen, nb), f32), V((scen, nl), i32), V((scen, nl), f32), V((scen, nl), f32), V((rows, LANES), f32),
             V((scen, rows, LANES), i32), V((scen, rows, LANES), f32), V((scen, btiles, LANES), f32), V((scen, 1, LANES), f32),
-            V((ranks, 2, rows, LANES), i32), V((ranks, 3, rows, LANES), f32), V((ranks, rows, LANES), i32),
+            V((2, ranks, rows, LANES), i32), V((ranks, 2, rows, LANES), f32), V((ranks, 1, rows, LANES), f32),
+            V((ranks, rows, LANES), i32),
             V((ranks, 2, nb), f32), V((ranks, 2, nb), f32), V((ranks, 2, LANES), f32), V((groups, SUB, LANES), f32),
             V((ranks, 2, nb), f32), V((ranks, rows, LANES), f32), V((ranks, btiles, LANES), f32), V((ranks, 1, LANES), f32),
             V((4, tiles, LANES), f32), V((2, ranks * rows, LANES), i32), V((3, ranks * rows, LANES), f32),
-            V((ranks * rows, LANES), i32), V((ranks * rows, LANES), f32), V((ranks * rows, LANES), f32), V((6 * high, SPAN), f32),
-            V((ranks, 2, nb), f32), V((ranks, btiles, LANES), f32), V((ranks, rows, LANES), f32),
+            V((ranks * rows, LANES), i32), V((4, ranks * rows, LANES), f32), V((ranks * rows, LANES), f32),
+            V((2, ranks * rows // SUB, SPAN // LANES, SUB * LANES, LANES), jnp.bfloat16), V((6 * high, SPAN), f32),
             V((ranks, 2, nb), f32), V((ranks, btiles, LANES), f32), V((ranks, rows, LANES), f32),
             V((ranks, 1, LANES), f32), V((groups, 1, LANES), f32),
             pltpu.SemaphoreType.DMA((15,)),
@@ -463,7 +534,23 @@
         *(x.reshape(rows, LANES) for x in (from_bus, to_bus, conduct, suscept, charging, rating)),
         status, slack, zdual,
     )))
-    return (mis, dual, lim, norms, tot[0])
+    mis, dual, lim, norms, tot = pl.pallas_call(
+        write_out,
+        out_shape=(
+            jax.ShapeDtypeStruct((scen, 2, nb), f32),
+            jax.ShapeDtypeStruct((scen, nb), f32),
+            jax.ShapeDtypeStruct((scen, nl), f32),
+            jax.ShapeDtypeStruct((4, scen), f32),
+            jax.ShapeDtypeStruct((1, 4), f32),
+        ),
+        in_specs=[vmem] * 5,
+        out_specs=(pl.BlockSpec(memory_space=pl.ANY),) * 5,
+        scratch_shapes=[
+            V((scen, nb), f32), V((scen, nl), f32), V((4, scen), f32), pltpu.SemaphoreType.DMA((5,)),
+        ],
+        compiler_params=pltpu.CompilerParams(vmem_limit_bytes=8 << 20),
+    )(*outs)
+    return (mis, dual, lim, norms.T, tot[0])
 
 
 def solution(mesh):

time: 47.4 us -> 44 us (0.928)
  local copies, waits for them, and re-layouts: 3.04 us -> 0 us
    unnamed x5 -> x0, local copies, waits for them, and re-layouts: 3.04 us -> none
    pallas_call x1, Pallas kernels: 43.6 us -> 42.5 us  [per_device(): pl.pallas_call(functools.partial(body, groups, ranks), out_shape=(jax.Sha...]
    pallas_call x0 -> x1, Pallas kernels: none -> 0.72 us  [per_device(): pl.pallas_call(write_out, out_shape=(jax.ShapeDtypeStruct((scen, 2, nb),...]
where the time goes in v2:
time: 44 us; the launch traced here: 43.9 us
  Pallas kernels  43.3 us (98%)
  between operations  0.65 us (1%)
    pallas_call x1, Pallas kernels, per_device(): pl.pallas_call(functools.partial(body, groups, ranks), out_shape=(jax.Sha...  42.5 us

profile of v2, /device:TPU:1, one launch (start us, length us, event | category | flops | bytes accessed | tf_op | source)
XLA Modules:
  0.0 43.9 jit_solution(15910805340996242354)
XLA Ops:
  0.6 42.5 %shard_map.182 = (f32[8,2,1280]{2,1,0:T(2,128)S(1)}, f32[8,10,128]{2,1,0:T(8,128)S(1)}, f32[8,13,128]{2,1,0:T(8,128)S(1)}, f32[8,128]{1,0:T(8,128)S(1)}, f32[1,4]{1,0:T(1,128)S(1)}) custom-call(f32[1,40]{1,0:T(1,128)} %bitcast.16, f32[1,40]{1,0:T(1,128)} %bitcast.17, f32[8,2,1280]{2,1,0:T(2,128)} %delta_any.1, f32[8,2,1280]{2,1,0:T(2,128)} %mult_any.1, ...), custom_call_target="tpu_custom_call" | custom-call | tf_op jit(solution)/shard_map/pallas_call | solution.py:500
  43.2 0.7 %shard_map.183 = (f32[8,2,1280]{2,1,0:T(2,128)}, f32[8,1280]{1,0:T(8,128)}, f32[8,1664]{1,0:T(8,128)}, f32[4,8]{1,0:T(4,128)}, f32[1,4]{1,0:T(1,128)}) custom-call(f32[8,2,1280]{2,1,0:T(2,128)S(1)} %get-tuple-element.15.min_, f32[8,10,128]{2,1,0:T(8,128)S(1)} %get-tuple-element.16.din, f32[8,13,128]{2,1,0:T(8,128)S(1)} %get-tuple-element.17.lin, ...), custom_call_target="tpu_custom_call" | custom-call | tf_op jit(solution)/shard_map/pallas_call | solution.py:537

commit v3 on v2

--- a/solution.py
+++ b/solution.py
@@ -36,13 +36,16 @@
     min_, din, lin, norm_out, tot_out,
     vm1, va1, dstg, mstg, nstg, ang8, st8, sl8, zd8, rate,
     ststg, wstg, astg, cstg,
-    ebuf, pbuf0, pbuf1, stbuf, mbuf, dbuf, zbuf, cbuf, nbuf, wbuf, abuf, compbuf,
+    pstg, pown, pz, pall, ebuf, stbuf, mbuf, dbuf, zbuf, cbuf, nbuf, wbuf, abuf, compbuf,
     table, dends, dpar, dst, dmult, dlim, hot, acc,
     mout, dout, lout, sqbuf, rowbuf,
-    local, send, recv,
+    local, send, recv, ends_recv, ends_recv2,
 ):
     grp, me = lax.axis_index("ctg"), lax.axis_index("br")
     core = lax.rem(grp, 2)
+    shares = pown.shape[0]
+    line = lax.rem(grp, groups // (shares // 2)) - core
+    part = 2 * (grp // (groups // (shares // 2))) + core
     sibling = grp + 1 - 2 * core
     scen, _, nb = delta_any.shape
     rows = from_any.shape[0]
@@ -56,24 +59,10 @@
         copy.start()
         return copy
 
-    ends_in = [pltpu.make_async_copy(src, ebuf.at[i, me], local.at[2 + i]) for i, src in enumerate((from_any, to_any))]
-    params_in = [
-        pltpu.make_async_copy(src, dst, local.at[8 + i])
-        for i, (src, dst) in enumerate(((g_any, pbuf0.at[me, 0]), (h_any, pbuf0.at[me, 1]), (b_any, pbuf1.at[me, 0])))
-    ]
-
-    @pl.when(core == 0)
-    def _():
-        for copy in (ends_in[0], params_in[0], params_in[1]):
-            copy.start()
-
-    @pl.when(core == 1)
-    def _():
-        for copy in (ends_in[1], params_in[2]):
-            copy.start()
-
+    ends_in = [fetch(2, from_any, ebuf.at[0, me]), fetch(3, to_any, ebuf.at[1, me])]
     base_in = [fetch(0, vm_any, vm1), fetch(1, va_any, va1)]
     status_in = [fetch(4, status_any, st8), fetch(5, slack_any, sl8), fetch(6, zdual_any, zd8), fetch(7, rating_any, rate)]
+    params_in = [fetch(8, g_any, pstg.at[0]), fetch(9, b_any, pstg.at[1]), fetch(10, h_any, pstg.at[2])]
     bus_in = [fetch(11, delta_any, dstg), fetch(12, mult_any, mstg)]
     late_in = [fetch(13, net_any, nstg), fetch(14, ang_any, ang8)]
 
@@ -113,8 +102,14 @@
     comp = st8[...].astype(f32) * (zd8[...] * sl8[...] - 0.01)
     cstg[:, 0, :] = jnp.broadcast_to(jnp.sum(comp * comp, axis=1, keepdims=True), (scen, LANES))
 
-    for copy in bus_in + late_in:
+    for copy in ends_in + params_in + bus_in + late_in:
         copy.wait()
+    share = pown.shape[1]
+    for j in range(3 * rows):
+        q, r = j // rows, j % rows
+        pown[j // share, j % share : j % share + 1, :] = pstg[q, r : r + 1, :]
+    for j in range(3 * rows, pown.shape[0] * share):
+        pown[j // share, j % share : j % share + 1, :] = jnp.zeros((1, LANES), f32)
     for k in range(btiles):
         astg[:, k, :] = ang8[:, k * LANES : (k + 1) * LANES]
 
@@ -131,12 +126,6 @@
             src_ref=src, dst_ref=dst, send_sem=send.at[kind], recv_sem=recv.at[kind],
             device_id=(lax.rem(grp + step, groups), me), device_id_type=MESH,
         ).start()
-
-    def across(kind, ref):
-        return pltpu.make_async_remote_copy(
-            src_ref=ref, dst_ref=ref, send_sem=send.at[kind], recv_sem=recv.at[kind],
-            device_id=(sibling, me), device_id_type=MESH,
-        )
 
     def whole(kind, ref, n):
         part = ref.at[pl.ds(0, n)]
@@ -159,36 +148,24 @@
 
     to_near(PIECE, lambda p: zbuf.at[me], zbuf.at[me])
 
-    @pl.when(core == 0)
-    def _():
-        ends_in[0].wait()
-        to_near(ENDS, lambda p: ebuf.at[0, me], ebuf.at[0, me])
-
-    @pl.when(core == 1)
-    def _():
-        ends_in[1].wait()
-        to_near(ENDS, lambda p: ebuf.at[1, me], ebuf.at[1, me])
-
+    def send_ends(step, carry):
+        pltpu.make_async_remote_copy(
+            src_ref=ebuf.at[core, me], dst_ref=ebuf.at[core, me], send_sem=send.at[ENDS], recv_sem=ends_recv.at[ranks - step],
+            device_id=(grp, lax.rem(me + step, ranks)), device_id_type=MESH,
+        ).start()
+        return carry
+
+    lax.fori_loop(1, ranks, send_ends, 0)
+    to_near(PARAMS, lambda p: pown.at[part], pz.at[me])
     to_near(MULT, lambda p: mstg.at[p], mbuf.at[me])
     to_near(DELTA, lambda p: dstg.at[p], dbuf.at[me])
     to_near(STATUS, lambda p: ststg.at[p], stbuf.at[me])
-
-    @pl.when(core == 0)
-    def _():
-        params_in[0].wait()
-        params_in[1].wait()
-        to_near(PARAMS, lambda p: pbuf0.at[me], pbuf0.at[me])
-
-    @pl.when(core == 1)
-    def _():
-        params_in[2].wait()
-        to_near(PARAMS, lambda p: pbuf1.at[me], pbuf1.at[me])
-
     to_near(COMP, lambda p: cstg.at[p], compbuf.at[me])
     to_near(NET, lambda p: nstg.at[p], nbuf.at[me])
     to_near(WORK, lambda p: wstg.at[p], wbuf.at[me])
     to_near(ANG, lambda p: astg.at[p], abuf.at[me])
 
+    pz[me] = pown[part]
     stbuf[me] = ststg[me]
     dbuf[me] = dstg[me]
     mbuf[me] = mstg[me]
@@ -197,6 +174,49 @@
     abuf[me] = astg[me]
     compbuf[me] = cstg[me]
     acc[...] = jnp.zeros_like(acc)
+
+    source = [lax.rem(me + j, ranks) for j in range(ranks)]
+    chunks = dends.shape[1] // SUB
+    high = acc.shape[0] // 6
+    column0 = lax.broadcasted_iota(jnp.int32, (LANES, LANES), 1)
+    labels = [(column0 + k * LANES).astype(bf16) for k in range(SPAN // LANES)]
+    steps = lax.broadcasted_iota(jnp.int32, (high, LANES), 0).astype(bf16)
+
+    def at_rows(i):
+        return pl.ds(pl.multiple_of(i * SUB, SUB), SUB)
+
+    def spread(x, n):
+        return jnp.concatenate([jnp.broadcast_to(x, (2 * SUB, LANES)).astype(bf16)] * (n // (2 * SUB)), axis=0)
+
+    def make_hot(step):
+        origin = lax.rem(me + step, ranks)
+        for end in range(2):
+            low = ebuf[end, origin] & (SPAN - 1)
+            for r in range(rows):
+                spots = spread(low[r : r + 1, :], LANES).T
+                place = pl.ds(pl.multiple_of((step * rows + r) * LANES, LANES), LANES)
+                for k, label in enumerate(labels):
+                    hot[end, k, place, :] = jnp.where(spots == label, bf16(1), bf16(0))
+
+    def ends_copy(sems, half, origin, step):
+        return pltpu.make_async_remote_copy(
+            src_ref=ebuf.at[half, origin], dst_ref=ebuf.at[half, origin], send_sem=send.at[ENDS2], recv_sem=sems.at[step],
+            device_id=(sibling, me), device_id_type=MESH,
+        )
+
+    make_hot(0)
+
+    def turn(t):
+        return jnp.where(lax.rem(t, 2) == 1, (t + 1) // 2, ranks - t // 2)
+
+    def forward(t, carry):
+        step = turn(t)
+        origin = lax.rem(me + step, ranks)
+        ends_copy(ends_recv, core, origin, step).wait_recv()
+        ends_copy(ends_recv2, core, origin, step).start()
+        return carry
+
+    lax.fori_loop(1, ranks, forward, 0)
 
     whole(PIECE, zbuf, ranks - 1).wait_recv()
     window = (LANES // 2) * core
@@ -211,39 +231,29 @@
     cbuf[grp, 6:8, :] = jnp.zeros((2, LANES), f32)
     to_far(BASE, cbuf.at[grp], cbuf.at[grp])
 
-    for c in range(2):
-        @pl.when(core == c)
-        def _(c=c):
-            whole(ENDS, ebuf.at[c], ranks - 1).wait_recv()
-            across(ENDS2, ebuf.at[c]).start()
-            across(ENDS2, ebuf.at[1 - c]).wait_recv()
-
+    def arrive(t, carry):
+        step = turn(t)
+        ends_copy(ends_recv2, 1 - core, lax.rem(me + step, ranks), step).wait_recv()
+        make_hot(step)
+        return carry
+
+    lax.fori_loop(1, ranks, arrive, 0)
     for end in range(2):
-        for z in range(ranks):
-            dends[end, z * rows : (z + 1) * rows, :] = ebuf[end, z]
-
-    chunks = dends.shape[1] // SUB
-    high = acc.shape[0] // 6
-    column0 = lax.broadcasted_iota(jnp.int32, (LANES, LANES), 1)
-    labels = [(column0 + k * LANES).astype(bf16) for k in range(SPAN // LANES)]
-    steps = lax.broadcasted_iota(jnp.int32, (high, LANES), 0).astype(bf16)
-
-    def at_rows(i):
-        return pl.ds(pl.multiple_of(i * SUB, SUB), SUB)
-
-    def spread(x, n):
-        return jnp.concatenate([jnp.broadcast_to(x, (2 * SUB, LANES)).astype(bf16)] * (n // (2 * SUB)), axis=0)
-
-    def make_hot(i, carry):
-        for end in range(2):
-            low = dends[end, at_rows(i), :] & (SPAN - 1)
-            for r in range(SUB):
-                spots = spread(low[r : r + 1, :], LANES).T
-                for k, label in enumerate(labels):
-                    hot[end, i, k, r * LANES : (r + 1) * LANES, :] = jnp.where(spots == label, bf16(1), bf16(0))
-        return carry
-
-    lax.fori_loop(0, chunks, make_hot, 0)
+        for j in range(ranks):
+            dends[end, j * rows : (j + 1) * rows, :] = ebuf[end, source[j]]
+
+    whole(PARAMS, pz, ranks - 1).wait_recv()
+    pall[part] = pz[...]
+
+    def share_params(d, carry):
+        other = lax.rem(part + d, shares)
+        pltpu.make_async_remote_copy(
+            src_ref=pz, dst_ref=pall.at[part], send_sem=send.at[PARAMS2], recv_sem=recv.at[PARAMS2],
+            device_id=((other // 2) * (groups // (shares // 2)) + line + lax.rem(other, 2), me), device_id_type=MESH,
+        ).start()
+        return carry
+
+    lax.fori_loop(1, shares, share_params, 0)
 
     whole(MULT, mbuf, ranks - 1).wait_recv()
     for z in range(ranks):
@@ -281,25 +291,14 @@
         keep(chunks - 1)
 
     whole(STATUS, stbuf, ranks - 1).wait_recv()
-    for z in range(ranks):
-        dst[z * rows : (z + 1) * rows, :] = stbuf[z]
-
-    @pl.when(core == 0)
-    def _():
-        whole(PARAMS, pbuf0, ranks - 1).wait_recv()
-        across(PARAMS2, pbuf0).start()
-        across(PARAMS2, pbuf1).wait_recv()
-
-    @pl.when(core == 1)
-    def _():
-        whole(PARAMS, pbuf1, ranks - 1).wait_recv()
-        across(PARAMS2, pbuf1).start()
-        across(PARAMS2, pbuf0).wait_recv()
-
-    for z in range(ranks):
-        dpar[0, z * rows : (z + 1) * rows, :] = pbuf0[z, 0]
-        dpar[1, z * rows : (z + 1) * rows, :] = pbuf1[z, 0]
-        dpar[2, z * rows : (z + 1) * rows, :] = pbuf0[z, 1]
+    for j in range(ranks):
+        dst[j * rows : (j + 1) * rows, :] = stbuf[source[j]]
+
+    whole(PARAMS2, pall, shares - 1).wait_recv()
+    for j in range(ranks):
+        for k in range(3 * rows):
+            q, r = k // rows, j * rows + k % rows
+            dpar[q, r : r + 1, :] = pall[k // share, source[j], k % share : k % share + 1, :]
 
     whole(DELTA, dbuf, ranks - 1).wait_recv()
     whole(BASE, cbuf, groups - 1).wait_recv()
@@ -345,7 +344,8 @@
                 lefts.append(jnp.concatenate(
                     [jnp.where(mask, spread(x[row, :], high), bf16(0)) for x in parts], axis=0
                 ))
-            right = jnp.concatenate([hot[end, i, k] for k in range(SPAN // LANES)], axis=1)
+            spots = pl.ds(pl.multiple_of(i * (SUB * LANES), SUB * LANES), SUB * LANES)
+            right = jnp.concatenate([hot[end, k, spots, :] for k in range(SPAN // LANES)], axis=1)
             dot = lax.dot_general(
                 jnp.concatenate(lefts, axis=1), right, (((1,), (0,)), ((), ())), preferred_element_type=f32
             )
@@ -394,8 +394,9 @@
                         dout[z, k : k + 1, :] = one
                         dual_sq = dual_sq + one * one
     lim_sq = jnp.zeros((rows, LANES), f32)
-    for z in range(ranks):
-        lim = stbuf[z].astype(f32) * (dlim[z * rows : (z + 1) * rows, :] + wbuf[z])
+    for j in range(ranks):
+        z = source[j]
+        lim = stbuf[z].astype(f32) * (dlim[j * rows : (j + 1) * rows, :] + wbuf[z])
         lout[z] = lim
         lim_sq = lim_sq + lim * lim
     comp_sq = jnp.zeros((1, LANES), f32)
@@ -433,18 +434,9 @@
     whole(LIM, lin, ranks - 1).wait_recv()
 
     whole(ENDS, ebuf.at[0], ranks - 1).wait_send()
-    across(ENDS2, ebuf.at[0]).wait_send()
-
-    @pl.when(core == 0)
-    def _():
-        whole(PARAMS, pbuf0, ranks - 1).wait_send()
-        across(PARAMS2, pbuf0).wait_send()
-
-    @pl.when(core == 1)
-    def _():
-        whole(PARAMS, pbuf1, ranks - 1).wait_send()
-        across(PARAMS2, pbuf1).wait_send()
-
+    whole(ENDS2, ebuf.at[0], ranks - 1).wait_send()
+    whole(PARAMS, pown, ranks - 1).wait_send()
+    whole(PARAMS2, pall, shares - 1).wait_send()
     for kind, ref in (
         (PIECE, zbuf), (STATUS, ststg), (DELTA, dstg), (MULT, mstg), (COMP, cstg), (NET, nstg), (WORK, wstg),
         (ANG, astg), (SQ, sqbuf), (MIS, mout), (DUAL, dout), (LIM, lout),
@@ -493,6 +485,8 @@
     tiles = buses // LANES
     high = -(-(buses // SPAN) // 16) * 16
     block = base_vm.shape[0]
+    shares = 8
+    share = -(-3 * rows // shares)
     f32, i32 = jnp.float32, jnp.int32
     vmem = pl.BlockSpec(memory_space=pltpu.VMEM)
     hbm = pl.BlockSpec(memory_space=pltpu.HBM)
@@ -513,18 +507,21 @@
             V((scen, 2, nb), f32), V((scen, 2, nb), f32), V((scen, 2, nb), f32),
             V((scen, nb), f32), V((scen, nl), i32), V((scen, nl), f32), V((scen, nl), f32), V((rows, LANES), f32),
             V((scen, rows, LANES), i32), V((scen, rows, LANES), f32), V((scen, btiles, LANES), f32), V((scen, 1, LANES), f32),
-            V((2, ranks, rows, LANES), i32), V((ranks, 2, rows, LANES), f32), V((ranks, 1, rows, LANES), f32),
+            V((3, rows, LANES), f32), V((shares, share, LANES), f32), V((ranks, share, LANES), f32),
+            V((shares, ranks, share, LANES), f32), V((2, ranks, rows, LANES), i32),
             V((ranks, rows, LANES), i32),
             V((ranks, 2, nb), f32), V((ranks, 2, nb), f32), V((ranks, 2, LANES), f32), V((groups, SUB, LANES), f32),
             V((ranks, 2, nb), f32), V((ranks, rows, LANES), f32), V((ranks, btiles, LANES), f32), V((ranks, 1, LANES), f32),
             V((4, tiles, LANES), f32), V((2, ranks * rows, LANES), i32), V((3, ranks * rows, LANES), f32),
             V((ranks * rows, LANES), i32), V((4, ranks * rows, LANES), f32), V((ranks * rows, LANES), f32),
-            V((2, ranks * rows // SUB, SPAN // LANES, SUB * LANES, LANES), jnp.bfloat16), V((6 * high, SPAN), f32),
+            V((2, SPAN // LANES, ranks * nl, LANES), jnp.bfloat16), V((6 * high, SPAN), f32),
             V((ranks, 2, nb), f32), V((ranks, btiles, LANES), f32), V((ranks, rows, LANES), f32),
             V((ranks, 1, LANES), f32), V((groups, 1, LANES), f32),
             pltpu.SemaphoreType.DMA((15,)),
             pltpu.SemaphoreType.DMA((KINDS,)),
             pltpu.SemaphoreType.DMA((KINDS,)),
+            pltpu.SemaphoreType.DMA((ranks,)),
+            pltpu.SemaphoreType.DMA((ranks,)),
         ],
         compiler_params=pltpu.CompilerParams(
             collective_id=0, has_side_effects=True, vmem_limit_bytes=40 << 20

time: 44 us -> 42.6 us (0.968)
  Pallas kernels: 43.3 us -> 41.9 us
    pallas_call x1, Pallas kernels: 42.5 us -> 41.1 us  [per_device(): pl.pallas_call(functools.partial(body, groups, ranks), out_shape=(jax.Sha...]
where the time goes in v3:
time: 42.6 us; the launch traced here: 42.5 us
  Pallas kernels  41.9 us (98%)
  between operations  0.65 us (2%)
    pallas_call x1, Pallas kernels, per_device(): pl.pallas_call(functools.partial(body, groups, ranks), out_shape=(jax.Sha...  41.1 us

profile of v3, /device:TPU:1, one launch (start us, length us, event | category | flops | bytes accessed | tf_op | source)
XLA Modules:
  0.0 42.5 jit_solution(2222961136158325893)
XLA Ops:
  0.6 41.1 %shard_map.182 = (f32[8,2,1280]{2,1,0:T(2,128)S(1)}, f32[8,10,128]{2,1,0:T(8,128)S(1)}, f32[8,13,128]{2,1,0:T(8,128)S(1)}, f32[8,128]{1,0:T(8,128)S(1)}, f32[1,4]{1,0:T(1,128)S(1)}) custom-call(f32[1,40]{1,0:T(1,128)} %bitcast.16, f32[1,40]{1,0:T(1,128)} %bitcast.17, f32[8,2,1280]{2,1,0:T(2,128)} %delta_any.1, f32[8,2,1280]{2,1,0:T(2,128)} %mult_any.1, ...), custom_call_target="tpu_custom_call" | custom-call | tf_op jit(solution)/shard_map/pallas_call | solution.py:494
  41.8 0.7 %shard_map.183 = (f32[8,2,1280]{2,1,0:T(2,128)}, f32[8,1280]{1,0:T(8,128)}, f32[8,1664]{1,0:T(8,128)}, f32[4,8]{1,0:T(4,128)}, f32[1,4]{1,0:T(1,128)}) custom-call(f32[8,2,1280]{2,1,0:T(2,128)S(1)} %get-tuple-element.15.min_, f32[8,10,128]{2,1,0:T(8,128)S(1)} %get-tuple-element.16.din, f32[8,13,128]{2,1,0:T(8,128)S(1)} %get-tuple-element.17.lin, ...), custom_call_target="tpu_custom_call" | custom-call | tf_op jit(solution)/shard_map/pallas_call | solution.py:534

commit v4 on v3

--- a/solution.py
+++ b/solution.py
@@ -37,7 +37,7 @@
     vm1, va1, dstg, mstg, nstg, ang8, st8, sl8, zd8, rate,
     ststg, wstg, astg, cstg,
     pstg, pown, pz, pall, ebuf, stbuf, mbuf, dbuf, zbuf, cbuf, nbuf, wbuf, abuf, compbuf,
-    table, dends, dpar, dst, dmult, dlim, hot, acc,
+    table, split, dends, dpar, dst, dmult, dlim, hot, acc,
     mout, dout, lout, sqbuf, rowbuf,
     local, send, recv, ends_recv, ends_recv2,
 ):
@@ -59,7 +59,7 @@
         copy.start()
         return copy
 
-    ends_in = [fetch(2, from_any, ebuf.at[0, me]), fetch(3, to_any, ebuf.at[1, me])]
+    ends_in = [fetch(2, from_any, ebuf.at[me, 0]), fetch(3, to_any, ebuf.at[me, 1])]
     base_in = [fetch(0, vm_any, vm1), fetch(1, va_any, va1)]
     status_in = [fetch(4, status_any, st8), fetch(5, slack_any, sl8), fetch(6, zdual_any, zd8), fetch(7, rating_any, rate)]
     params_in = [fetch(8, g_any, pstg.at[0]), fetch(9, b_any, pstg.at[1]), fetch(10, h_any, pstg.at[2])]
@@ -148,14 +148,17 @@
 
     to_near(PIECE, lambda p: zbuf.at[me], zbuf.at[me])
 
-    def send_ends(step, carry):
-        pltpu.make_async_remote_copy(
-            src_ref=ebuf.at[core, me], dst_ref=ebuf.at[core, me], send_sem=send.at[ENDS], recv_sem=ends_recv.at[ranks - step],
-            device_id=(grp, lax.rem(me + step, ranks)), device_id_type=MESH,
-        ).start()
-        return carry
-
-    lax.fori_loop(1, ranks, send_ends, 0)
+    @pl.when(core == 1)
+    def _():
+        def send_ends(step, carry):
+            pltpu.make_async_remote_copy(
+                src_ref=ebuf.at[me], dst_ref=ebuf.at[me], send_sem=send.at[ENDS], recv_sem=ends_recv.at[ranks - step],
+                device_id=(grp, lax.rem(me + step, ranks)), device_id_type=MESH,
+            ).start()
+            return carry
+
+        lax.fori_loop(1, ranks, send_ends, 0)
+
     to_near(PARAMS, lambda p: pown.at[part], pz.at[me])
     to_near(MULT, lambda p: mstg.at[p], mbuf.at[me])
     to_near(DELTA, lambda p: dstg.at[p], dbuf.at[me])
@@ -191,32 +194,39 @@
     def make_hot(step):
         origin = lax.rem(me + step, ranks)
         for end in range(2):
-            low = ebuf[end, origin] & (SPAN - 1)
+            low = ebuf[origin, end] & (SPAN - 1)
             for r in range(rows):
                 spots = spread(low[r : r + 1, :], LANES).T
                 place = pl.ds(pl.multiple_of((step * rows + r) * LANES, LANES), LANES)
                 for k, label in enumerate(labels):
                     hot[end, k, place, :] = jnp.where(spots == label, bf16(1), bf16(0))
 
-    def ends_copy(sems, half, origin, step):
+    def ends_copy(sems, origin, step):
         return pltpu.make_async_remote_copy(
-            src_ref=ebuf.at[half, origin], dst_ref=ebuf.at[half, origin], send_sem=send.at[ENDS2], recv_sem=sems.at[step],
+            src_ref=ebuf.at[origin], dst_ref=ebuf.at[origin], send_sem=send.at[ENDS2], recv_sem=sems.at[step],
             device_id=(sibling, me), device_id_type=MESH,
         )
 
     make_hot(0)
 
-    def turn(t):
-        return jnp.where(lax.rem(t, 2) == 1, (t + 1) // 2, ranks - t // 2)
-
-    def forward(t, carry):
-        step = turn(t)
+    def arrive(t, carry):
+        step = jnp.where(lax.rem(t, 2) == 1, (t + 1) // 2, ranks - t // 2)
         origin = lax.rem(me + step, ranks)
-        ends_copy(ends_recv, core, origin, step).wait_recv()
-        ends_copy(ends_recv2, core, origin, step).start()
+
+        @pl.when(core == 1)
+        def _():
+            ends_copy(ends_recv, origin, step).wait_recv()
+            ends_copy(ends_recv2, origin, step).start()
+
+        @pl.when(core == 0)
+        def _():
+            ends_copy(ends_recv2, origin, step).wait_recv()
+
+        make_hot(step)
         return carry
 
-    lax.fori_loop(1, ranks, forward, 0)
+    early = 3
+    lax.fori_loop(1, early, arrive, 0)
 
     whole(PIECE, zbuf, ranks - 1).wait_recv()
     window = (LANES // 2) * core
@@ -231,16 +241,10 @@
     cbuf[grp, 6:8, :] = jnp.zeros((2, LANES), f32)
     to_far(BASE, cbuf.at[grp], cbuf.at[grp])
 
-    def arrive(t, carry):
-        step = turn(t)
-        ends_copy(ends_recv2, 1 - core, lax.rem(me + step, ranks), step).wait_recv()
-        make_hot(step)
-        return carry
-
-    lax.fori_loop(1, ranks, arrive, 0)
+    lax.fori_loop(early, ranks, arrive, 0)
     for end in range(2):
         for j in range(ranks):
-            dends[end, j * rows : (j + 1) * rows, :] = ebuf[end, source[j]]
+            dends[end, j * rows : (j + 1) * rows, :] = ebuf[source[j], end]
 
     whole(PARAMS, pz, ranks - 1).wait_recv()
     pall[part] = pz[...]
@@ -262,43 +266,65 @@
                 at = z * btiles + k
                 table[2 + q, at : at + 1, :] = mbuf[z, q : q + 1, k * LANES : (k + 1) * LANES]
 
+    for q in range(2):
+        x = table[2 + q]
+        top = x.astype(bf16)
+        split[q * tiles : (q + 1) * tiles, 0:LANES] = top
+        split[q * tiles : (q + 1) * tiles, LANES : 2 * LANES] = (x - top.astype(f32)).astype(bf16)
+
+    def pick_end(i, end, first):
+        spot = dends[end, at_rows(i), :]
+        low, tile = spot & (LANES - 1), spot >> 7
+        found = [jnp.zeros((SUB, LANES), f32) for _ in range(2)]
+        for k in range(tiles):
+            here = tile == k
+            for q in range(2):
+                row = jnp.broadcast_to(table[first + q, k : k + 1, :], (SUB, LANES))
+                got = jnp.take_along_axis(row, low, axis=1, mode="promise_in_bounds")
+                found[q] = jnp.where(here, got, found[q])
+        return found
+
     def pick(i, first):
-        picked = []
-        for end in range(2):
-            spot = dends[end, at_rows(i), :]
-            low, tile = spot & (LANES - 1), spot >> 7
-            found = [jnp.zeros((SUB, LANES), f32) for _ in range(2)]
-            for k in range(tiles):
-                here = tile == k
+        return tuple(pick_end(i, 0, first) + pick_end(i, 1, first))
+
+    lane_row = lax.broadcasted_iota(jnp.int32, (LANES, LANES), 0).astype(bf16)
+    sublane = lax.broadcasted_iota(jnp.int32, (SUB, LANES), 0)
+
+    def pick_by_matmul(i, end):
+        spot = dends[end, at_rows(i), :]
+        low, tile = spot & (LANES - 1), spot >> 7
+        found = [[], []]
+        for r in range(0, SUB, 2):
+            ones = jnp.concatenate(
+                [jnp.where(spread(low[k : k + 1, :], LANES) == lane_row, bf16(1), bf16(0)) for k in (r, r + 1)], axis=1
+            )
+            got = jnp.dot(split[...], jnp.concatenate([ones, ones], axis=0), preferred_element_type=f32)
+            for k in range(2):
+                at = jnp.broadcast_to(tile[r + k : r + k + 1, :], (SUB, LANES)) - sublane
+                sums = [jnp.zeros((SUB, LANES), f32) for _ in range(2)]
+                for j in range(tiles // SUB):
+                    here = at == j * SUB
+                    for q in range(2):
+                        top = q * tiles + j * SUB
+                        sums[q] = jnp.where(here, got[top : top + SUB, k * LANES : (k + 1) * LANES], sums[q])
                 for q in range(2):
-                    row = jnp.broadcast_to(table[first + q, k : k + 1, :], (SUB, LANES))
-                    got = jnp.take_along_axis(row, low, axis=1, mode="promise_in_bounds")
-                    found[q] = jnp.where(here, got, found[q])
-            picked += found
-        return tuple(picked)
+                    found[q].append(jnp.sum(sums[q], axis=0, keepdims=True))
+        return [jnp.concatenate(x, axis=0) for x in found]
 
     def keep(i):
-        for k, x in enumerate(pick(i, 2)):
+        for k, x in enumerate(pick_end(i, 0, 2) + pick_by_matmul(i, 1)):
             dmult[k, at_rows(i), :] = x
 
-    def keep_two(j, carry):
-        keep(2 * j)
-        keep(2 * j + 1)
+    unit = 4
+
+    def keep_unit(j, carry):
+        for k in range(unit):
+            keep(unit * j + k)
         return carry
 
-    lax.fori_loop(0, chunks // 2, keep_two, 0)
-    if chunks % 2:
-        keep(chunks - 1)
-
-    whole(STATUS, stbuf, ranks - 1).wait_recv()
-    for j in range(ranks):
-        dst[j * rows : (j + 1) * rows, :] = stbuf[source[j]]
-
-    whole(PARAMS2, pall, shares - 1).wait_recv()
-    for j in range(ranks):
-        for k in range(3 * rows):
-            q, r = k // rows, j * rows + k % rows
-            dpar[q, r : r + 1, :] = pall[k // share, source[j], k % share : k % share + 1, :]
+    lax.fori_loop(0, chunks // unit, keep_unit, 0)
+    for i in range(chunks // unit * unit, chunks):
+        keep(i)
 
     whole(DELTA, dbuf, ranks - 1).wait_recv()
     whole(BASE, cbuf, groups - 1).wait_recv()
@@ -364,6 +390,17 @@
         return following
 
     first = pick(0, 0)
+
+    whole(STATUS, stbuf, ranks - 1).wait_recv()
+    for j in range(ranks):
+        dst[j * rows : (j + 1) * rows, :] = stbuf[source[j]]
+
+    whole(PARAMS2, pall, shares - 1).wait_recv()
+    for j in range(ranks):
+        for k in range(3 * rows):
+            q, r = k // rows, j * rows + k % rows
+            dpar[q, r : r + 1, :] = pall[k // share, source[j], k % share : k % share + 1, :]
+
     following = two(1)
     acc[...] += scatter(0, first)
     scatter_two(chunks - 2, lax.fori_loop(1, chunks // 2, advance, following))
@@ -433,8 +470,11 @@
     whole(DUAL, din, ranks - 1).wait_recv()
     whole(LIM, lin, ranks - 1).wait_recv()
 
-    whole(ENDS, ebuf.at[0], ranks - 1).wait_send()
-    whole(ENDS2, ebuf.at[0], ranks - 1).wait_send()
+    @pl.when(core == 1)
+    def _():
+        whole(ENDS, ebuf, ranks - 1).wait_send()
+        whole(ENDS2, ebuf, ranks - 1).wait_send()
+
     whole(PARAMS, pown, ranks - 1).wait_send()
     whole(PARAMS2, pall, shares - 1).wait_send()
     for kind, ref in (
@@ -508,11 +548,11 @@
             V((scen, nb), f32), V((scen, nl), i32), V((scen, nl), f32), V((scen, nl), f32), V((rows, LANES), f32),
             V((scen, rows, LANES), i32), V((scen, rows, LANES), f32), V((scen, btiles, LANES), f32), V((scen, 1, LANES), f32),
             V((3, rows, LANES), f32), V((shares, share, LANES), f32), V((ranks, share, LANES), f32),
-            V((shares, ranks, share, LANES), f32), V((2, ranks, rows, LANES), i32),
+            V((shares, ranks, share, LANES), f32), V((ranks, 2, rows, LANES), i32),
             V((ranks, rows, LANES), i32),
             V((ranks, 2, nb), f32), V((ranks, 2, nb), f32), V((ranks, 2, LANES), f32), V((groups, SUB, LANES), f32),
             V((ranks, 2, nb), f32), V((ranks, rows, LANES), f32), V((ranks, btiles, LANES), f32), V((ranks, 1, LANES), f32),
-            V((4, tiles, LANES), f32), V((2, ranks * rows, LANES), i32), V((3, ranks * rows, LANES), f32),
+            V((4, tiles, LANES), f32), V((2 * tiles, 2 * LANES), jnp.bfloat16), V((2, ranks * rows, LANES), i32), V((3, ranks * rows, LANES), f32),
             V((ranks * rows, LANES), i32), V((4, ranks * rows, LANES), f32), V((ranks * rows, LANES), f32),
             V((2, SPAN // LANES, ranks * nl, LANES), jnp.bfloat16), V((6 * high, SPAN), f32),
             V((ranks, 2, nb), f32), V((ranks, btiles, LANES), f32), V((ranks, rows, LANES), f32),

time: 42.6 us -> 39 us (0.915)
  Pallas kernels: 41.9 us -> 38.2 us
    pallas_call x1, Pallas kernels: 41.1 us -> 37.5 us  [per_device(): pl.pallas_call(functools.partial(body, groups, ranks), out_shape=(jax.Sha...]
where the time goes in v4:
time: 39 us; the launch traced here: 38.9 us
  Pallas kernels  38.2 us (98%)
  between operations  0.65 us (2%)
    pallas_call x1, Pallas kernels, per_device(): pl.pallas_call(functools.partial(body, groups, ranks), out_shape=(jax.Sha...  37.5 us

profile of v4, /device:TPU:1, one launch (start us, length us, event | category | flops | bytes accessed | tf_op | source)
XLA Modules:
  0.0 38.9 jit_solution(1979135419016485051)
XLA Ops:
  0.6 37.5 %shard_map.182 = (f32[8,2,1280]{2,1,0:T(2,128)S(1)}, f32[8,10,128]{2,1,0:T(8,128)S(1)}, f32[8,13,128]{2,1,0:T(8,128)S(1)}, f32[8,128]{1,0:T(8,128)S(1)}, f32[1,4]{1,0:T(1,128)S(1)}) custom-call(f32[1,40]{1,0:T(1,128)} %bitcast.16, f32[1,40]{1,0:T(1,128)} %bitcast.17, f32[8,2,1280]{2,1,0:T(2,128)} %delta_any.1, f32[8,2,1280]{2,1,0:T(2,128)} %mult_any.1, ...), custom_call_target="tpu_custom_call" | custom-call | tf_op jit(solution)/shard_map/pallas_call | solution.py:534
  38.1 0.7 %shard_map.183 = (f32[8,2,1280]{2,1,0:T(2,128)}, f32[8,1280]{1,0:T(8,128)}, f32[8,1664]{1,0:T(8,128)}, f32[4,8]{1,0:T(4,128)}, f32[1,4]{1,0:T(1,128)}) custom-call(f32[8,2,1280]{2,1,0:T(2,128)S(1)} %get-tuple-element.15.min_, f32[8,10,128]{2,1,0:T(8,128)S(1)} %get-tuple-element.16.din, f32[8,13,128]{2,1,0:T(8,128)S(1)} %get-tuple-element.17.lin, ...), custom_call_target="tpu_custom_call" | custom-call | tf_op jit(solution)/shard_map/pallas_call | solution.py:574

commit v5 on v4

--- a/solution.py
+++ b/solution.py
@@ -39,7 +39,7 @@
     pstg, pown, pz, pall, ebuf, stbuf, mbuf, dbuf, zbuf, cbuf, nbuf, wbuf, abuf, compbuf,
     table, split, dends, dpar, dst, dmult, dlim, hot, acc,
     mout, dout, lout, sqbuf, rowbuf,
-    local, send, recv, ends_recv, ends_recv2,
+    send, recv, ends_recv, ends_recv2,
 ):
     grp, me = lax.axis_index("ctg"), lax.axis_index("br")
     core = lax.rem(grp, 2)
@@ -55,7 +55,7 @@
     piece_len = vm_any.shape[1]
 
     def fetch(i, src, dst):
-        copy = pltpu.make_async_copy(src, dst, local.at[i])
+        copy = pltpu.make_async_copy(src, dst, send.at[i])
         copy.start()
         return copy
 
@@ -68,16 +68,16 @@
 
     barrier = pltpu.get_barrier_semaphore()
 
-    def greet_near(i, carry):
-        pl.semaphore_signal(barrier, inc=1, device_id=(grp, lax.rem(me + i, ranks)), device_id_type=MESH)
-        return carry
-
-    def greet_far(i, carry):
-        pl.semaphore_signal(barrier, inc=1, device_id=(lax.rem(grp + i, groups), me), device_id_type=MESH)
-        return carry
-
-    lax.fori_loop(1, ranks, greet_near, 0)
-    lax.fori_loop(1, groups, greet_far, 0)
+    def outward(n):
+        return [n // 2 + ((i + 1) // 2 if i % 2 else -(i // 2)) for i in range(n - 1)]
+
+    near_steps = outward(ranks)
+    near_peers = {step: lax.rem(me + step, ranks) for step in near_steps}
+
+    for step in near_steps:
+        pl.semaphore_signal(barrier, inc=1, device_id=(grp, near_peers[step]), device_id_type=MESH)
+    for step in outward(groups):
+        pl.semaphore_signal(barrier, inc=1, device_id=(lax.rem(grp + step, groups), me), device_id_type=MESH)
 
     for copy in base_in + status_in:
         copy.wait()
@@ -118,7 +118,7 @@
     def near(kind, step, src, dst):
         pltpu.make_async_remote_copy(
             src_ref=src, dst_ref=dst, send_sem=send.at[kind], recv_sem=recv.at[kind],
-            device_id=(grp, lax.rem(me + step, ranks)), device_id_type=MESH,
+            device_id=(grp, near_peers[step]), device_id_type=MESH,
         ).start()
 
     def far(kind, step, src, dst):
@@ -135,16 +135,12 @@
         )
 
     def to_near(kind, src_of, dst):
-        def go(step, carry):
-            near(kind, step, src_of(lax.rem(me + step, ranks)), dst)
-            return carry
-        lax.fori_loop(1, ranks, go, 0)
+        for step in near_steps:
+            near(kind, step, src_of(near_peers[step]), dst)
 
     def to_far(kind, src, dst):
-        def go(step, carry):
+        for step in outward(groups):
             far(kind, step, src, dst)
-            return carry
-        lax.fori_loop(1, groups, go, 0)
 
     to_near(PIECE, lambda p: zbuf.at[me], zbuf.at[me])
 
@@ -163,10 +159,6 @@
     to_near(MULT, lambda p: mstg.at[p], mbuf.at[me])
     to_near(DELTA, lambda p: dstg.at[p], dbuf.at[me])
     to_near(STATUS, lambda p: ststg.at[p], stbuf.at[me])
-    to_near(COMP, lambda p: cstg.at[p], compbuf.at[me])
-    to_near(NET, lambda p: nstg.at[p], nbuf.at[me])
-    to_near(WORK, lambda p: wstg.at[p], wbuf.at[me])
-    to_near(ANG, lambda p: astg.at[p], abuf.at[me])
 
     pz[me] = pown[part]
     stbuf[me] = ststg[me]
@@ -238,13 +230,9 @@
             found = jnp.where(inside, zbuf[b], found)
         cbuf[grp, m : m + 1, :] = found[0:1, :]
         cbuf[grp, 3 + m : 4 + m, :] = found[1:2, :]
-    cbuf[grp, 6:8, :] = jnp.zeros((2, LANES), f32)
     to_far(BASE, cbuf.at[grp], cbuf.at[grp])
 
-    lax.fori_loop(early, ranks, arrive, 0)
-    for end in range(2):
-        for j in range(ranks):
-            dends[end, j * rows : (j + 1) * rows, :] = ebuf[source[j], end]
+    lax.fori_loop(early, ranks - 2, arrive, 0)
 
     whole(PARAMS, pz, ranks - 1).wait_recv()
     pall[part] = pz[...]
@@ -258,6 +246,11 @@
         return carry
 
     lax.fori_loop(1, shares, share_params, 0)
+
+    lax.fori_loop(ranks - 2, ranks, arrive, 0)
+    for end in range(2):
+        for j in range(ranks):
+            dends[end, j * rows : (j + 1) * rows, :] = ebuf[source[j], end]
 
     whole(MULT, mbuf, ranks - 1).wait_recv()
     for z in range(ranks):
@@ -286,6 +279,11 @@
 
     def pick(i, first):
         return tuple(pick_end(i, 0, first) + pick_end(i, 1, first))
+
+    to_near(COMP, lambda p: cstg.at[p], compbuf.at[me])
+    to_near(NET, lambda p: nstg.at[p], nbuf.at[me])
+    to_near(WORK, lambda p: wstg.at[p], wbuf.at[me])
+    to_near(ANG, lambda p: astg.at[p], abuf.at[me])
 
     lane_row = lax.broadcasted_iota(jnp.int32, (LANES, LANES), 0).astype(bf16)
     sublane = lax.broadcasted_iota(jnp.int32, (SUB, LANES), 0)
@@ -550,14 +548,13 @@
             V((3, rows, LANES), f32), V((shares, share, LANES), f32), V((ranks, share, LANES), f32),
             V((shares, ranks, share, LANES), f32), V((ranks, 2, rows, LANES), i32),
             V((ranks, rows, LANES), i32),
-            V((ranks, 2, nb), f32), V((ranks, 2, nb), f32), V((ranks, 2, LANES), f32), V((groups, SUB, LANES), f32),
+            V((ranks, 2, nb), f32), V((ranks, 2, nb), f32), V((ranks, 2, LANES), f32), V((groups, 6, LANES), f32),
             V((ranks, 2, nb), f32), V((ranks, rows, LANES), f32), V((ranks, btiles, LANES), f32), V((ranks, 1, LANES), f32),
             V((4, tiles, LANES), f32), V((2 * tiles, 2 * LANES), jnp.bfloat16), V((2, ranks * rows, LANES), i32), V((3, ranks * rows, LANES), f32),
             V((ranks * rows, LANES), i32), V((4, ranks * rows, LANES), f32), V((ranks * rows, LANES), f32),
             V((2, SPAN // LANES, ranks * nl, LANES), jnp.bfloat16), V((6 * high, SPAN), f32),
             V((ranks, 2, nb), f32), V((ranks, btiles, LANES), f32), V((ranks, rows, LANES), f32),
             V((ranks, 1, LANES), f32), V((groups, 1, LANES), f32),
-            pltpu.SemaphoreType.DMA((15,)),
             pltpu.SemaphoreType.DMA((KINDS,)),
             pltpu.SemaphoreType.DMA((KINDS,)),
             pltpu.SemaphoreType.DMA((ranks,)),

time: 39 us -> 38.6 us (0.990)
  Pallas kernels: 38.2 us -> 37.8 us
    pallas_call x1, Pallas kernels: 37.5 us -> 37.1 us  [per_device(): pl.pallas_call(functools.partial(body, groups, ranks), out_shape=(jax.Sha...]
where the time goes in v5:
time: 38.6 us; the launch traced here: 38.4 us
  Pallas kernels  37.8 us (98%)
  between operations  0.65 us (2%)
    pallas_call x1, Pallas kernels, per_device(): pl.pallas_call(functools.partial(body, groups, ranks), out_shape=(jax.Sha...  37.1 us

profile of v5, /device:TPU:1, one launch (start us, length us, event | category | flops | bytes accessed | tf_op | source)
XLA Modules:
  0.0 38.4 jit_solution(4315034355087839176)
XLA Ops:
  0.6 37.1 %shard_map.182 = (f32[8,2,1280]{2,1,0:T(2,128)S(1)}, f32[8,10,128]{2,1,0:T(8,128)S(1)}, f32[8,13,128]{2,1,0:T(8,128)S(1)}, f32[8,128]{1,0:T(8,128)S(1)}, f32[1,4]{1,0:T(1,128)S(1)}) custom-call(f32[1,40]{1,0:T(1,128)} %bitcast.16, f32[1,40]{1,0:T(1,128)} %bitcast.17, f32[8,2,1280]{2,1,0:T(2,128)} %delta_any.1, f32[8,2,1280]{2,1,0:T(2,128)} %mult_any.1, ...), custom_call_target="tpu_custom_call" | custom-call | tf_op jit(solution)/shard_map/pallas_call | solution.py:532
  37.7 0.7 %shard_map.183 = (f32[8,2,1280]{2,1,0:T(2,128)}, f32[8,1280]{1,0:T(8,128)}, f32[8,1664]{1,0:T(8,128)}, f32[4,8]{1,0:T(4,128)}, f32[1,4]{1,0:T(1,128)}) custom-call(f32[8,2,1280]{2,1,0:T(2,128)S(1)} %get-tuple-element.15.min_, f32[8,10,128]{2,1,0:T(8,128)S(1)} %get-tuple-element.16.din, f32[8,13,128]{2,1,0:T(8,128)S(1)} %get-tuple-element.17.lin, ...), custom_call_target="tpu_custom_call" | custom-call | tf_op jit(solution)/shard_map/pallas_call | solution.py:571
